TPU v7x, 32 devices: a whole 2x2x4 slice. The times are simulated.
32 devices in a mesh: dp: 8 (over z, x), mp: 4 (over y, core).
Axes of the slice: x: 2, y: 2, z: 4, core: 2. Of those that a mesh axis runs over, the one named last changes fastest.
Arguments:
- sparse_vecs: bfloat16 [8192, 26, 128], P(('dp', 'mp')), may hold values from -6 to 6
- dense_vec: bfloat16 [8192, 128], P(('dp', 'mp')), may hold values from -6 to 6
- top_cot: bfloat16 [8192, 1024], P(('dp', 'mp')), may hold values from -0.59765625 to 0.59765625
- top_weight: bfloat16 [479, 1024], replicated, may hold values from -0.25 to 0.25
- owner_ids: int32 [8192, 26, 1], P(('dp', 'mp')), may hold values from 0 to 7; in each aligned block of 6656 rows (0 to 6655, 6656 to 13311, ..., all dimensions but the last counted through in order) at most 1664 rows name the same one
- local_rows: int32 [8192, 26], P(('dp', 'mp')), may hold values from 0 to 127
- table: float32 [26, 1024, 128], P(None, ('dp', 'mp')), may hold values from -0.6 to 0.6
- accum: float32 [26, 1024], P(None, ('dp', 'mp')), may hold values from 0.05 to 2
Outputs:
- dense_grad: bfloat16 [8192, 128], P(('dp', 'mp'))
- new_table: float32 [26, 1024, 128], P(None, ('dp', 'mp'))
- new_accum: float32 [26, 1024], P(None, ('dp', 'mp'))
Inputs may be any that keep to these rules, and one draw needn't show every extreme that they name: `owner_ids`: among the lookups of one device's 256 samples no owner group is named more than 1664 times; in every draw some device names some owner group exactly 1664 times.
All inputs are finite; a program needn't handle non-finite values.
Results may differ from a plain program's by a relative error of at most 0.005.
Values may be sent and summed in bfloat16 or wider, within the bound.
No kernel may reach another device: no remote copies, remote signals or barrier semaphores. Data moves between devices by JAX's collectives and lax.ppermute only.
A program may use at most 128 MiB of HBM per device.

v0:
```python
import jax
import jax.numpy as jnp
import numpy as np
from jax import lax
from jax.sharding import PartitionSpec as P

LEARN_RATE = 0.1
EPSILON = 1e-08


def pair_matrix(feature_count):
    row_index, col_index = np.tril_indices(feature_count, -1)
    pair_count = row_index.shape[0]
    matrix = np.zeros((pair_count, feature_count * feature_count), np.float32)
    matrix[np.arange(pair_count), row_index * feature_count + col_index] = 1.0
    matrix[np.arange(pair_count), col_index * feature_count + row_index] = 1.0
    return jnp.asarray(matrix)


def accumulate(grad_rows, grad_keys, first_col, columns):
    sources, capacity, row_width = grad_rows.shape
    most_rows = max(1, 4096 // capacity)
    per_turn = 1
    while per_turn * 2 <= most_rows and sources % (per_turn * 2) == 0:
        per_turn = per_turn * 2
    turn_count = sources // per_turn
    row_blocks = grad_rows.reshape(turn_count, per_turn * capacity, row_width)
    key_blocks = grad_keys.reshape(turn_count, per_turn * capacity) - first_col
    targets = jnp.arange(columns, dtype=jnp.int32)[None, :]

    def add_block(turn_index, running):
        row_piece = lax.dynamic_index_in_dim(row_blocks, turn_index, 0, keepdims=False)
        key_piece = lax.dynamic_index_in_dim(key_blocks, turn_index, 0, keepdims=False)
        onehot = (key_piece[:, None] == targets).astype(jnp.bfloat16)
        return running + lax.dot_general(
            onehot, row_piece, (((0,), (0,)), ((), ())), preferred_element_type=jnp.float32
        )

    return lax.fori_loop(0, turn_count, add_block, jnp.zeros((columns, row_width), jnp.float32))


def slot_ranks(target, dp_count):
    lookups = target.shape[0]
    block_len = min(512, lookups)
    block_count = (lookups + block_len - 1) // block_len
    padded_len = block_count * block_len
    padded_target = jnp.concatenate([target, jnp.full((padded_len - lookups,), -1, jnp.int32)])
    member = (padded_target[:, None] == jnp.arange(dp_count, dtype=jnp.int32)[None, :]).astype(
        jnp.bfloat16
    )
    member_blocks = member.reshape(block_count, block_len, dp_count)
    lower = (jnp.arange(block_len)[:, None] >= jnp.arange(block_len)[None, :]).astype(jnp.bfloat16)
    within = jnp.einsum("ij,bjd->bid", lower, member_blocks, preferred_element_type=jnp.float32)
    block_totals = within[:, block_len - 1, :]
    strict = (jnp.arange(block_count)[:, None] > jnp.arange(block_count)[None, :]).astype(
        jnp.float32
    )
    offsets = jnp.dot(
        strict, block_totals, precision=lax.Precision.HIGHEST, preferred_element_type=jnp.float32
    )
    counts = (within + offsets[:, None, :]) * member_blocks.astype(jnp.float32)
    ranks = jnp.sum(counts, axis=2).reshape(padded_len)
    return ranks.astype(jnp.int32) - 1


def per_device(sparse_vecs, dense_vec, top_cot, top_weight, owner_ids, local_rows, table, accum):
    batch_rows, table_count, row_width = sparse_vecs.shape
    feature_count = table_count + 1
    input_cot = jnp.einsum("bh,zh->bz", top_cot, top_weight, preferred_element_type=jnp.float32)
    symmetric = jnp.dot(
        input_cot[:, row_width:],
        pair_matrix(feature_count),
        precision=lax.Precision.HIGHEST,
        preferred_element_type=jnp.float32,
    )
    symmetric = symmetric.reshape(batch_rows, feature_count, feature_count)
    features = jnp.concatenate([dense_vec[:, None, :], sparse_vecs], axis=1).astype(jnp.float32)
    feature_grad = jnp.einsum("bij,bje->bie", symmetric, features, precision=lax.Precision.HIGHEST)
    dense_grad = (input_cot[:, :row_width] + feature_grad[:, 0]).astype(jnp.bfloat16)
    sparse_grad = feature_grad[:, 1:].astype(jnp.bfloat16)
    dp_count = lax.axis_size("dp")
    rows_own = table.shape[1]
    own_cols = table_count * rows_own
    lookups = batch_rows * table_count
    capacity = 2 * lookups // dp_count
    slot_total = dp_count * capacity
    target = owner_ids.reshape(lookups)
    table_pos = jnp.arange(table_count, dtype=jnp.int32)[None, :]
    column = (
        local_rows // rows_own * own_cols + table_pos * rows_own + local_rows % rows_own
    ).reshape(lookups)
    slot_index = target * capacity + slot_ranks(target, dp_count)
    source_of = (
        jnp.full((slot_total,), -1, jnp.int32)
        .at[slot_index]
        .set(jnp.arange(lookups, dtype=jnp.int32))
    )
    filled = source_of >= 0
    safe_source = jnp.maximum(source_of, 0)
    send_rows = jnp.take(sparse_grad.reshape(lookups, row_width), safe_source, axis=0)
    send_rows = jnp.where(filled[:, None], send_rows, jnp.zeros_like(send_rows))
    send_keys = jnp.where(filled, jnp.take(column, safe_source, axis=0), -1)
    send_rows = send_rows.reshape(dp_count, capacity, row_width)
    send_keys = send_keys.reshape(dp_count, capacity)
    recv_rows, recv_keys = (
        lax.all_to_all(send_rows, "dp", split_axis=0, concat_axis=0, tiled=True),
        lax.all_to_all(send_keys, "dp", split_axis=0, concat_axis=0, tiled=True),
    )
    row_grad = lax.psum_scatter(
        accumulate(recv_rows, recv_keys, jnp.int32(0), lax.axis_size("mp") * own_cols).astype(
            jnp.bfloat16
        ),
        "mp",
        scatter_dimension=0,
        tiled=True,
    ).astype(jnp.float32)
    row_grad = row_grad.reshape(table_count, rows_own, row_width)
    new_accum = accum + jnp.mean(row_grad * row_grad, axis=-1)
    new_table = table - LEARN_RATE * row_grad / (jnp.sqrt(new_accum)[:, :, None] + EPSILON)
    return (dense_grad, new_table, new_accum)


def solution(mesh):
    in_specs = (
        P(("dp", "mp"), None, None),
        P(("dp", "mp"), None),
        P(("dp", "mp"), None),
        P(),
        P(("dp", "mp"), None, None),
        P(("dp", "mp"), None),
        P(None, ("dp", "mp"), None),
        P(None, ("dp", "mp")),
    )
    out_specs = (P(("dp", "mp"), None), P(None, ("dp", "mp"), None), P(None, ("dp", "mp")))
    return jax.shard_map(
        per_device, mesh=mesh, in_specs=in_specs, out_specs=out_specs, check_vma=False
    )
```

profile of v0, /device:TPU:0, one launch (start us, length us, event | category | flops | bytes accessed | tf_op | source)
XLA Modules:
  0.0 365.2 jit_solution(838342878156029762)
XLA Ops:
  7.2 0.0 copy-start
  7.2 0.8 broadcast_multiply_fusion
  8.0 0.9 copy.33
  8.9 0.8 fusion.22
  9.7 0.1 copy.36
  9.8 0.1 reshape.121
  10.0 0.1 copy.32
  10.1 0.2 mul.48
  10.3 0.1 eq.60
  10.4 0.3 convolution_bitcast_fusion
  10.7 0.1 slice.28
  10.8 0.1 copy.34
  10.9 0.1 fusion.30
  11.0 0.2 multiply_reduce_fusion
  11.3 0.1 fusion.27
  11.4 24.9 %scatter_custom_fusion = s32[13312]{0:T(1024)S(1)} fusion(s32[6656]{0:T(1024)S(1)} %fusion.27, s32[6656]{0:T(1024)S(1)} %iota.39, s32[]{:T(128)} %constant.98.clone.1), kind=kCustom, calls=%fused_computation.53 | custom fusion | bytes 53252 | tf_op jit(solution)/shard_map/scatter | solution.py:96
  36.3 0.0 copy-start.2
  36.3 73.7 %gather_fusion = s32[13312]{0:T(1024)S(1)} fusion(s32[6656]{0:T(1024)S(1)} %reshape.121, s32[13312]{0:T(1024)S(1)} %maximum_clamp_fusion), kind=kCustom, calls=%fused_computation | custom fusion | bytes 159744 | tf_op jit(solution)/shard_map/jit(_take)/gather | solution.py:102
  110.0 0.6 select_select_fusion.1
  110.6 7.3 %all-to-all-start = ((s32[8,1,1664]{2,1,0:T(1,128)}), s32[8,1,1664]{2,1,0:T(1,128)S(1)}, u32[]{:S(2)}, u32[]{:S(2)}) async-start(s32[8,1,1664]{2,1,0:T(1,128)} %bitcast.5), calls=%async_computation | async-start | bytes 106496 | tf_op jit(solution)/shard_map/all_to_all | solution.py:107
  117.9 0.0 copy-done
  117.9 0.0 copy-done.2
  117.9 0.5 fusion.33
  118.4 3.3 fusion.15
  121.6 0.1 reshape.120
  121.7 4.4 %copy.30 = f32[256,27,27]{2,1,0:T(8,128)} copy(f32[256,27,27]{0,2,1:T(8,128)S(1)} %reshape.120) | data formatting | bytes 1492992 | tf_op jit(solution)/shard_map/reshape | solution.py:76
  126.2 0.0 copy-start.4
  126.2 2.6 copy.29
  128.8 0.0 copy-done.4
  128.8 0.1 copy.28
  129.0 4.5 %fusion.8 = f32[256,27,128]{2,1,0:T(8,128)S(1)} fusion(f32[256,27,27]{2,1,0:T(8,128)} %copy.30, bf16[256,26,128]{2,1,0:T(8,128)(2,1)S(1)} %copy.29, bf16[256,1,128]{2,1,0:T(2,128)(2,1)S(1)} %copy.28), kind=kOutput, calls=%fused_computation.14 | convolution fusion | flops 290193408 | bytes 6054912 | tf_op jit(solution)/shard_map/bij,bje->bie/dot_general | solution.py:78
  133.5 0.0 copy-start.1
  133.5 1.9 copy-done.1
  135.4 1.9 slice.36
  137.2 2.6 reshape.123
  139.8 46.8 %gather_fusion.1 = bf16[13312,128]{1,0:T(8,128)(2,1)} fusion(bf16[6656,128]{1,0:T(8,128)(2,1)S(1)} %reshape.123, s32[13312]{0:T(1024)S(1)} %maximum_clamp_fusion), kind=kCustom, calls=%fused_computation.1 | custom fusion | bytes 6868992 | tf_op jit(solution)/shard_map/jit(_take)/gather | solution.py:100
  186.6 0.1 broadcast_in_dim.65
  186.6 0.1 broadcast_in_dim.63
  186.7 7.0 %select_select_fusion = bf16[8,1664,128]{2,1,0:T(8,128)(2,1)} fusion(bf16[8,1664,128]{2,1,0:T(8,128)(2,1)} %bitcast.35, pred[8,1664]{1,0:T(8,128)(4,1)S(1)} %broadcast_in_dim.65, pred[8,1664]{1,0:T(8,128)(4,1)S(1)} %broadcast_in_dim.63), kind=kLoop, calls=%fused_computation.13 | loop fusion | flops 3407872 | bytes 6842368 | tf_op jit(solution)/shard_map/jit(_where)/select_n | solution.py:101
  193.7 0.0 all-to-all-done
  193.8 6.0 %all-to-all-start.1 = ((bf16[8,1664,128]{2,1,0:T(8,128)(2,1)}), bf16[8,1664,128]{2,1,0:T(8,128)(2,1)}, u32[]{:S(2)}, u32[]{:S(2)}) async-start(bf16[8,1664,128]{2,1,0:T(8,128)(2,1)} %select_select_fusion), calls=%async_computation.1 | async-start | bytes 6815744 | tf_op jit(solution)/shard_map/all_to_all | solution.py:106
  199.8 0.0 reduce-scatter.2.cloned.1.call-start
  199.8 0.1 reduce.3
  200.0 75.6 %all-to-all-done.1 = bf16[8,1664,128]{2,1,0:T(8,128)(2,1)} async-done(((bf16[8,1664,128]{2,1,0:T(8,128)(2,1)}), bf16[8,1664,128]{2,1,0:T(8,128)(2,1)}, u32[]{:S(2)}, u32[]{:S(2)}) %all-to-all-start.1) | async-done | bytes 3407904 | tf_op jit(solution)/shard_map/all_to_all | solution.py:106
  275.6 56.1 %while.14 = (s32[]{:T(128)}, f32[3328,128]{1,0:T(8,128)S(1)}, s32[4,3328]{1,0:T(4,128)S(1)}, bf16[4,3328,128]{2,1,0:T(8,128)(2,1)}, s32[]{:T(128)}, /*index=5*/s32[]{:T(128)}) while((s32[]{:T(128)}, f32[3328,128]{1,0:T(8,128)S(1)}, s32[4,3328]{1,0:T(4,128)S(1)}, bf16[4,3328,128]{2,1,0:T(8,128)(2,1)}, s32[]{:T(128)}, ...), condition=%wide.region_3.4_spmd.clone, body=%wide.region_2.3_spmd.clone.sunk | while | flops 2847277056 | bytes 4299871 | solution.py:39
  275.7 14.0 %fusion.41 = f32[3328,128]{1,0:T(8,128)S(1)} fusion(s32[3328]{0:T(1024)S(1)} %dynamic-slice_reduce_fusion.2, f32[3328,128]{1,0:T(8,128)S(1)} %get-tuple-element.171, bf16[4,3328,128]{2,1,0:T(8,128)(2,1)} %get-tuple-element.179, s32[]{:T(128)S(6)} %copy.43, pred[]{:T(512)S(6)} %compare.6), kind=kOutput, calls=%fused_computation.7.clone.1 | convolution fusion | flops 2847277056 | bytes 4273157 | tf_op jit(solution)/shard_map/while/body/eval_jaxpr/dot_general | solution.py:35
  289.7 14.0 %fusion.41 = f32[3328,128]{1,0:T(8,128)S(1)} fusion(s32[3328]{0:T(1024)S(1)} %dynamic-slice_reduce_fusion.2, f32[3328,128]{1,0:T(8,128)S(1)} %get-tuple-element.171, bf16[4,3328,128]{2,1,0:T(8,128)(2,1)} %get-tuple-element.179, s32[]{:T(128)S(6)} %copy.43, pred[]{:T(512)S(6)} %compare.6), kind=kOutput, calls=%fused_computation.7.clone.1 | convolution fusion | flops 2847277056 | bytes 4273157 | tf_op jit(solution)/shard_map/while/body/eval_jaxpr/dot_general | solution.py:35
  303.7 14.0 %fusion.41 = f32[3328,128]{1,0:T(8,128)S(1)} fusion(s32[3328]{0:T(1024)S(1)} %dynamic-slice_reduce_fusion.2, f32[3328,128]{1,0:T(8,128)S(1)} %get-tuple-element.171, bf16[4,3328,128]{2,1,0:T(8,128)(2,1)} %get-tuple-element.179, s32[]{:T(128)S(6)} %copy.43, pred[]{:T(512)S(6)} %compare.6), kind=kOutput, calls=%fused_computation.7.clone.1 | convolution fusion | flops 2847277056 | bytes 4273157 | tf_op jit(solution)/shard_map/while/body/eval_jaxpr/dot_general | solution.py:35
  317.8 14.0 %fusion.41 = f32[3328,128]{1,0:T(8,128)S(1)} fusion(s32[3328]{0:T(1024)S(1)} %dynamic-slice_reduce_fusion.2, f32[3328,128]{1,0:T(8,128)S(1)} %get-tuple-element.171, bf16[4,3328,128]{2,1,0:T(8,128)(2,1)} %get-tuple-element.179, s32[]{:T(128)S(6)} %copy.43, pred[]{:T(512)S(6)} %compare.6), kind=kOutput, calls=%fused_computation.7.clone.1 | convolution fusion | flops 2847277056 | bytes 4273157 | tf_op jit(solution)/shard_map/while/body/eval_jaxpr/dot_general | solution.py:35
  331.7 0.0 copy-start.5
  331.7 1.0 convert_element_type.38
  332.7 0.0 copy-start.3
  332.7 0.0 reduce-scatter.2.cloned.1.call-update
  332.8 1.3 slice.27
  334.1 0.1 copy.39
  334.2 0.7 copy.37
  335.0 20.7 %reduce-scatter.2.cloned.1.call-done = bf16[832,128]{1,0:T(8,128)(2,1)} async-done(((bf16[3328,128]{1,0:T(8,128)(2,1)}), bf16[832,128]{1,0:T(8,128)(2,1)}) %reduce-scatter.2.cloned.1.call-update) | async-done | bytes 213008 | tf_op jit(solution)/shard_map/reduce_scatter | solution.py:109
  355.6 1.1 fusion.14
  356.8 0.1 div.34
  356.8 0.0 copy-done.5
  356.8 0.6 sqrt_add_fusion
  357.5 0.0 copy-done.3
  357.5 0.9 divide_subtract_fusion
  (13 shorter events, 0.3 us)
Async XLA Ops:
  7.2 110.7 %copy-start = (bf16[479,1024]{1,0:T(8,128)(2,1)S(1)}, bf16[479,1024]{1,0:T(8,128)(2,1)}, u32[]{:S(2)}) copy-start(bf16[479,1024]{1,0:T(8,128)(2,1)} %param.14) | copy-start | bytes 2942980
  36.3 81.6 %copy-start.2 = (bf16[256,1024]{1,0:T(8,128)(2,1)S(1)}, bf16[256,1024]{1,0:T(8,128)(2,1)}, u32[]{:S(2)}) copy-start(bf16[256,1024]{1,0:T(8,128)(2,1)} %param.13) | copy-start | bytes 1572868
  110.6 83.1 %all-to-all-start = ((s32[8,1,1664]{2,1,0:T(1,128)}), s32[8,1,1664]{2,1,0:T(1,128)S(1)}, u32[]{:S(2)}, u32[]{:S(2)}) async-start(s32[8,1,1664]{2,1,0:T(1,128)} %bitcast.5), calls=%async_computation | async-start | bytes 106496 | tf_op jit(solution)/shard_map/all_to_all | solution.py:107
  126.2 2.6 copy-start.4
  133.5 1.9 copy-start.1
  193.8 81.9 %all-to-all-start.1 = ((bf16[8,1664,128]{2,1,0:T(8,128)(2,1)}), bf16[8,1664,128]{2,1,0:T(8,128)(2,1)}, u32[]{:S(2)}, u32[]{:S(2)}) async-start(bf16[8,1664,128]{2,1,0:T(8,128)(2,1)} %select_select_fusion), calls=%async_computation.1 | async-start | bytes 6815744 | tf_op jit(solution)/shard_map/all_to_all | solution.py:106
  199.8 155.9 %reduce-scatter.2.cloned.1.call-start = ((), (), s32[]{:S(2)}) async-start(), calls=%async_computation.3 | async-start | bytes 1064960 | tf_op jit(solution)/shard_map/reduce_scatter | solution.py:109
  331.7 25.1 %copy-start.5 = (f32[26,32]{1,0:T(8,128)S(1)}, f32[26,32]{1,0:T(8,128)}, u32[]{:S(2)}) copy-start(f32[26,32]{1,0:T(8,128)} %param.18) | copy-start | bytes 9988
  332.7 24.7 %copy-start.3 = (f32[26,32,128]{2,1,0:T(8,128)S(1)}, f32[26,32,128]{2,1,0:T(8,128)}, u32[]{:S(2)}) copy-start(f32[26,32,128]{2,1,0:T(8,128)} %param.17) | copy-start | bytes 1277956
Sparse Core Ops, SparseCore 0:
  332.9 22.6 reduce-scatter.1
where the time goes:
time: 366 us; the launch traced here: 365 us
  local copies, waits for them, and re-layouts  163 us (45%)
  waiting for transfers between devices  96.3 us (26%)
  matrix products  64.4 us (18%)
  between operations  14.3 us (4%)
  other arithmetic  13.5 us (4%)
  starting transfers between devices  13.3 us (4%)
    all_to_all x1, waiting for transfers between devices, per_device(): lax.all_to_all(send_rows, 'dp', split_axis=0, concat_axis=0, tiled=True)  75.6 us
    gather x1, local copies, waits for them, and re-layouts, per_device(): send_keys = jnp.where(filled, jnp.take(column, safe_source, axis=0), -1)  73.7 us
    dot_general x4, matrix products, add_block(): lax.dot_general(onehot, row_piece, (((0,), (0,)), ((), ())), preferred_el...  55.8 us
    gather x1, local copies, waits for them, and re-layouts, per_device(): jnp.take(sparse_grad.reshape(lookups, row_width), safe_source, axis=0)  46.8 us
    scatter x1, local copies, waits for them, and re-layouts, per_device(): source_of = jnp.full((slot_total,), -1, jnp.int32).at[slot_index].set(jnp...  24.9 us
    reduce_scatter x1, waiting for transfers between devices, per_device(): lax.psum_scatter(accumulate(recv_rows, recv_keys, jnp.int32(0), lax.axis_...  20.7 us
  transfers between devices with their start and end apart: 3, of which 2 were waited for; matrix products, arithmetic and copies ran while one was open for 21% of the time, Pallas kernels for 0%

commit v1 on v0

v1 whole, which is shorter than its diff:
```python
import jax
import jax.numpy as jnp
import numpy as np
from jax import lax
from jax.experimental import pallas as pl
from jax.experimental.pallas import tpu as pltpu
from jax.sharding import PartitionSpec as P

LEARN_RATE = 0.1
EPSILON = 1e-08


def symmetric_rows(feature_count):
    row_index, col_index = np.tril_indices(feature_count, -1)
    pair_count = row_index.shape[0]
    matrix = np.zeros((feature_count, feature_count, pair_count), np.float32)
    matrix[row_index, col_index, np.arange(pair_count)] = 1.0
    matrix[col_index, row_index, np.arange(pair_count)] = 1.0
    return jnp.asarray(matrix.reshape(feature_count * feature_count, pair_count), jnp.bfloat16)


def interaction(sparse_vecs, dense_vec, top_cot, top_weight):
    batch_rows, table_count, row_width = sparse_vecs.shape
    feature_count = table_count + 1
    expanded = jnp.dot(
        symmetric_rows(feature_count), top_weight[row_width:], preferred_element_type=jnp.float32
    ).astype(jnp.bfloat16)
    direct = jnp.einsum(
        "bh,zh->bz", top_cot, top_weight[:row_width], preferred_element_type=jnp.float32
    )
    symmetric = jnp.einsum("bh,zh->bz", top_cot, expanded, preferred_element_type=jnp.float32)
    symmetric = symmetric.reshape(batch_rows, feature_count, feature_count)
    features = jnp.concatenate([dense_vec[:, None, :], sparse_vecs], axis=1).astype(jnp.float32)
    feature_grad = jnp.einsum("bij,bje->bie", symmetric, features, precision=lax.Precision.HIGHEST)
    dense_grad = (direct + feature_grad[:, 0]).astype(jnp.bfloat16)
    sparse_grad = feature_grad[:, 1:].astype(jnp.bfloat16)
    return dense_grad, sparse_grad


def sum_kernel(ids_ref, rows_ref, out_ref):
    sources = rows_ref.shape[0]
    blocks, _, block_rows, width = out_ref.shape
    samples = rows_ref.shape[2]
    base = pl.program_id(1) * (blocks * block_rows)
    target = lax.broadcasted_iota(jnp.int32, (blocks * block_rows, samples), 0) + base
    total = jnp.zeros((blocks * block_rows, width), jnp.float32)
    for s in range(sources):
        onehot = (target == ids_ref[s, 0]).astype(jnp.float32).astype(jnp.bfloat16)
        total = total + jnp.dot(onehot, rows_ref[s, 0], preferred_element_type=jnp.float32)
    out_ref[...] = total.reshape(blocks, 1, block_rows, width).astype(out_ref.dtype)


def sum_rows(ids, rows, blocks, block_rows, dtype):
    sources, tables, samples, width = rows.shape
    step = 4 if blocks % 4 == 0 else 1
    return pl.pallas_call(
        sum_kernel,
        grid=(tables, blocks // step),
        in_specs=[
            pl.BlockSpec((sources, 1, 1, samples), lambda t, h: (0, t, 0, 0)),
            pl.BlockSpec((sources, 1, samples, width), lambda t, h: (0, t, 0, 0)),
        ],
        out_specs=pl.BlockSpec((step, 1, block_rows, width), lambda t, h: (h, t, 0, 0)),
        out_shape=jax.ShapeDtypeStruct((blocks, tables, block_rows, width), dtype),
        cost_estimate=pl.CostEstimate(
            flops=2 * tables * sources * samples * blocks * block_rows * width,
            bytes_accessed=rows.size * 2 + blocks * tables * block_rows * width * 4,
            transcendentals=0,
        ),
    )(ids[:, :, None, :], rows)


def per_device(sparse_vecs, dense_vec, top_cot, top_weight, owner_ids, local_rows, table, accum):
    batch_rows, table_count, row_width = sparse_vecs.shape
    dp_count, mp_count = lax.axis_size("dp"), lax.axis_size("mp")
    rows_own = table.shape[1]
    group_rows = rows_own * mp_count
    per_mp = -(-table_count // mp_count)
    padding = per_mp * mp_count - table_count
    inner = 2 if dp_count % 2 == 0 else 1
    outer = dp_count // inner

    keys = (owner_ids[:, :, 0] * group_rows + local_rows).T
    keys = jnp.pad(keys, ((0, padding), (0, 0)), constant_values=-1)
    keys = lax.all_to_all(
        keys.reshape(mp_count, per_mp, batch_rows), "mp", split_axis=0, concat_axis=0, tiled=True
    )

    dense_grad, sparse_grad = interaction(sparse_vecs, dense_vec, top_cot, top_weight)
    send = jnp.pad(sparse_grad.transpose(1, 0, 2), ((0, padding), (0, 0), (0, 0)))
    rows = lax.all_to_all(
        send.reshape(mp_count, per_mp, batch_rows, row_width),
        "mp",
        split_axis=0,
        concat_axis=0,
        tiled=True,
    )

    owner, local = keys // group_rows, keys % group_rows
    place = owner // inner * group_rows + local
    part = owner % inner
    mine = lax.axis_index("dp") % inner
    total = sum_rows(
        jnp.where((keys >= 0) & (part == mine), place, -1), rows, outer, group_rows, jnp.float32
    )
    if inner == 2:
        other = sum_rows(
            jnp.where((keys >= 0) & (part != mine), place, -1),
            rows,
            outer,
            group_rows,
            jnp.bfloat16,
        )
        swap = [(i, i ^ 1) for i in range(dp_count)]
        total = total + lax.ppermute(other, "dp", swap).astype(jnp.float32)
    groups = [[r + inner * k for k in range(outer)] for r in range(inner)]
    parts = lax.all_to_all(
        total.astype(jnp.bfloat16),
        "dp",
        split_axis=0,
        concat_axis=0,
        axis_index_groups=groups,
        tiled=True,
    )
    summed = jnp.sum(parts.astype(jnp.float32), axis=0).astype(jnp.bfloat16)
    summed = summed.reshape(per_mp, mp_count, rows_own, row_width).transpose(1, 0, 2, 3)
    row_grad = lax.all_to_all(summed, "mp", split_axis=0, concat_axis=0, tiled=True)
    row_grad = row_grad.reshape(per_mp * mp_count, rows_own, row_width)[:table_count]
    row_grad = row_grad.astype(jnp.float32)
    new_accum = accum + jnp.mean(row_grad * row_grad, axis=-1)
    new_table = table - LEARN_RATE * row_grad / (jnp.sqrt(new_accum)[:, :, None] + EPSILON)
    return (dense_grad, new_table, new_accum)


def solution(mesh):
    in_specs = (
        P(("dp", "mp"), None, None),
        P(("dp", "mp"), None),
        P(("dp", "mp"), None),
        P(),
        P(("dp", "mp"), None, None),
        P(("dp", "mp"), None),
        P(None, ("dp", "mp"), None),
        P(None, ("dp", "mp")),
    )
    out_specs = (P(("dp", "mp"), None), P(None, ("dp", "mp"), None), P(None, ("dp", "mp")))
    return jax.shard_map(
        per_device, mesh=mesh, in_specs=in_specs, out_specs=out_specs, check_vma=False
    )
```

time: 366 us -> 122 us (0.33)
  local copies, waits for them, and re-layouts: 163 us -> 15.1 us
  matrix products: 64.4 us -> 9.1 us
  waiting for transfers between devices: 96.3 us -> 59.1 us
  between operations: 14.3 us -> 0.77 us
  Pallas kernels: 0 us -> 13.2 us
  other arithmetic: 13.5 us -> 5.53 us
  starting transfers between devices: 13.3 us -> 18.3 us
    gather x2 -> x0, local copies, waits for them, and re-layouts: 120 us -> none  [the longest x1 73.7 us: per_device(): send_keys = jnp.where(filled, jnp.take(column, safe_source, axis=0), -1)]
    dot_general x9 -> x3, matrix products: 64.4 us -> 9.1 us  [the longest x1 4.49 us: interaction(): jnp.einsum('bij,bje->bie', symmetric, features, precision=lax.Precision.H...]
    all_to_all x2 -> x4, waiting for transfers between devices: 75.7 us -> 46.2 us  [the longest x1 22.1 us: per_device(): lax.all_to_all(send.reshape(mp_count, per_mp, batch_rows, row_width), 'mp...]
    scatter x1 -> x0, local copies, waits for them, and re-layouts: 24.9 us -> none  [per_device(): source_of = jnp.full((slot_total,), -1, jnp.int32).at[slot_index].set(jnp...]
    reduce_scatter x1 -> x0, waiting for transfers between devices: 20.7 us -> none  [per_device(): lax.psum_scatter(accumulate(recv_rows, recv_keys, jnp.int32(0), lax.axis_...]
    pallas_call x0 -> x2, Pallas kernels: none -> 13.2 us  [sum_rows(): pl.pallas_call(sum_kernel, grid=(tables, blocks // step), in_specs=[pl.Bl...]
    ppermute x0 -> x1, waiting for transfers between devices: none -> 12.9 us  [per_device(): total = total + lax.ppermute(other, 'dp', swap).astype(jnp.float32)]
    select_n x3 -> x0, other arithmetic: 7.79 us -> none  [the longest x1 7.05 us: per_device(): send_rows = jnp.where(filled[:, None], send_rows, jnp.zeros_like(send_rows))]
  transfers between devices with their start and end apart: 3 -> 5, of which waited for: 2 -> 4; matrix products, arithmetic and copies ran while one was open for 21% -> 17% of each run, Pallas kernels for 0% -> 6%
where the time goes in v1:
time: 122 us; the launch traced here: 121 us
  waiting for transfers between devices  59.1 us (48%)
  starting transfers between devices  18.3 us (15%)
  local copies, waits for them, and re-layouts  15.1 us (12%)
  Pallas kernels  13.2 us (11%)
  matrix products  9.1 us (7%)
  other arithmetic  5.53 us (5%)
    all_to_all x1, waiting for transfers between devices, per_device(): lax.all_to_all(send.reshape(mp_count, per_mp, batch_rows, row_width), 'mp...  22.1 us
    all_to_all x1, waiting for transfers between devices, per_device(): lax.all_to_all(total.astype(jnp.bfloat16), 'dp', split_axis=0, concat_axi...  20.4 us
    pallas_call x2, Pallas kernels, sum_rows(): pl.pallas_call(sum_kernel, grid=(tables, blocks // step), in_specs=[pl.Bl...  13.2 us
    ppermute x1, waiting for transfers between devices, per_device(): total = total + lax.ppermute(other, 'dp', swap).astype(jnp.float32)  12.9 us
    all_to_all x1, starting transfers between devices, per_device(): lax.all_to_all(total.astype(jnp.bfloat16), 'dp', split_axis=0, concat_axi...  5.12 us
    reshape x2, local copies, waits for them, and re-layouts, interaction(): symmetric = symmetric.reshape(batch_rows, feature_count, feature_count)  4.56 us
    dot_general x1, matrix products, interaction(): jnp.einsum('bij,bje->bie', symmetric, features, precision=lax.Precision.H...  4.49 us
    unnamed x16, local copies, waits for them, and re-layouts  4.44 us
  transfers between devices with their start and end apart: 5, of which 4 were waited for; matrix products, arithmetic and copies ran while one was open for 17% of the time, Pallas kernels for 6%

profile of v1, /device:TPU:0, one launch (start us, length us, event | category | flops | bytes accessed | tf_op | source)
XLA Modules:
  0.0 121.1 jit_solution(16863351708699233029)
XLA Ops:
  0.6 0.0 copy-start
  0.6 0.8 fusion.16
  1.5 0.6 reshape.26
  2.1 4.3 %all-to-all-start = ((s32[4,7,256]{2,1,0:T(8,128)}), s32[4,7,256]{2,1,0:T(8,128)S(1)}, u32[]{:S(2)}, u32[]{:S(2)}) async-start(s32[4,7,256]{2,1,0:T(8,128)} %reshape.26), calls=%async_computation | async-start | bytes 65536 | tf_op jit(solution)/shard_map/all_to_all | solution.py:85
  6.4 0.0 copy-done
  6.4 2.7 %fusion.6 = f32[256,729]{0,1:T(8,128)S(1)} fusion(bf16[256,1024]{1,0:T(8,128)(2,1)S(1)} %copy-done, bf16[729,351]{1,0:T(8,128)(2,1)} %constant.77.clone, bf16[479,1024]{1,0:T(8,128)(2,1)} %param.12), kind=kOutput, calls=%fused_computation.9 | convolution fusion | flops 906992640 | bytes 2556928 | tf_op jit(solution)/shard_map/bh,zh->bz/dot_general | solution.py:31
  9.1 0.1 reshape.25
  9.2 0.0 copy-start.3
  9.2 4.5 %copy.39 = f32[256,27,27]{2,1,0:T(8,128)} copy(f32[256,27,27]{0,2,1:T(8,128)S(1)} %reshape.25) | data formatting | bytes 1492992 | tf_op jit(solution)/shard_map/reshape | solution.py:32
  13.7 0.0 copy-done.3
  13.7 0.0 copy-start.5
  13.7 1.1 copy.38
  14.8 0.0 copy-done.5
  14.8 0.1 copy.37
  14.9 4.5 %fusion.1 = f32[256,27,128]{2,1,0:T(8,128)S(1)} fusion(f32[256,27,27]{2,1,0:T(8,128)} %copy.39, bf16[256,26,128]{2,1,0:T(8,128)(2,1)S(1)} %copy.38, bf16[256,1,128]{2,1,0:T(2,128)(2,1)S(1)} %copy.37), kind=kOutput, calls=%fused_computation.2 | convolution fusion | flops 290193408 | bytes 6054912 | tf_op jit(solution)/shard_map/bij,bje->bie/dot_general | solution.py:34
  19.4 0.0 copy-start.1
  19.5 0.6 fusion
  20.0 1.4 %copy-done.1 = f32[256,27,128]{2,1,0:T(8,128)} copy-done((f32[256,27,128]{2,1,0:T(8,128)}, f32[256,27,128]{2,1,0:T(8,128)S(1)}, u32[]{:S(2)}) %copy-start.1) | copy-done | bytes 3538968
  21.4 0.7 copy.53
  22.1 1.5 %pad.9.clone = bf16[28,256,128]{2,1,0:T(8,128)(2,1)} pad(bf16[26,256,128]{2,1,0:T(8,128)(2,1)S(1)} %copy.53, bf16[]{:T(256)} %constant.72.clone.1), padding=0_2x0_0x0_0 | pad | bytes 3538946 | tf_op jit(solution)/shard_map/jit(_pad)/pad | solution.py:90
  23.5 0.0 all-to-all-done
  23.5 3.6 %all-to-all-start.1 = ((bf16[4,7,256,128]{3,2,1,0:T(8,128)(2,1)}), bf16[4,7,256,128]{3,2,1,0:T(8,128)(2,1)S(1)}, u32[]{:S(2)}, u32[]{:S(2)}) async-start(bf16[4,7,256,128]{3,2,1,0:T(8,128)(2,1)} %bitcast.29), calls=%async_computation.1 | async-start | bytes 3670016 | tf_op jit(solution)/shard_map/all_to_all | solution.py:91
  27.1 0.1 select_bitcast_fusion
  27.2 0.6 copy.46.ids_ref
  27.9 22.1 %all-to-all-done.1.rows_ref = bf16[4,7,256,128]{3,2,1,0:T(8,128)(2,1)S(1)} async-done(((bf16[4,7,256,128]{3,2,1,0:T(8,128)(2,1)}), bf16[4,7,256,128]{3,2,1,0:T(8,128)(2,1)S(1)}, u32[]{:S(2)}, u32[]{:S(2)}) %all-to-all-start.1) | async-done | bytes 1835040 | tf_op jit(solution)/shard_map/all_to_all | solution.py:91
  49.9 0.0 copy-start.2
  49.9 1.2 %copy-done.2 = bf16[4,7,256,128]{3,2,1,0:T(8,128)(2,1)} copy-done((bf16[4,7,256,128]{3,2,1,0:T(8,128)(2,1)}, bf16[4,7,256,128]{3,2,1,0:T(8,128)(2,1)S(1)}, u32[]{:S(2)}) %copy-start.2) | copy-done | bytes 1835032
  51.2 6.5 %shard_map.113 = bf16[4,7,128,128]{3,2,1,0:T(8,128)(2,1)} custom-call(s32[4,7,1,256]{3,2,1,0:T(1,128)} %copy.46.ids_ref, bf16[4,7,256,128]{3,2,1,0:T(8,128)(2,1)} %copy-done.2), custom_call_target="tpu_custom_call" | custom-call | flops 939524096 | bytes 3670016 | tf_op jit(solution)/shard_map/pallas_call | solution.py:56
  57.7 2.0 %collective-permute-start = (bf16[4,7,128,128]{3,2,1,0:T(8,128)(2,1)}, bf16[4,7,128,128]{3,2,1,0:T(8,128)(2,1)S(1)}, u32[]{:S(2)}, u32[]{:S(2)}) collective-permute-start(bf16[4,7,128,128]{3,2,1,0:T(8,128)(2,1)} %shard_map.113), channel_id=1, source_target_pairs={{0,4},{4,0},{8,12},{12,8},{16,20},{20,16},{24,28},{28,24},{1,5},{5... | collective-permute-start | bytes 2752520 | tf_op jit(solution)/shard_map/ppermute | solution.py:115
  59.7 0.1 select_bitcast_fusion.1
  59.7 0.6 copy.44.ids_ref
  60.4 6.7 %shard_map.112 = f32[4,7,128,128]{3,2,1,0:T(8,128)} custom-call(s32[4,7,1,256]{3,2,1,0:T(1,128)} %copy.44.ids_ref, bf16[4,7,256,128]{3,2,1,0:T(8,128)(2,1)} %copy-done.2), custom_call_target="tpu_custom_call" | custom-call | flops 939524096 | bytes 3670016 | tf_op jit(solution)/shard_map/pallas_call | solution.py:56
  67.0 12.9 %collective-permute-done = bf16[4,7,128,128]{3,2,1,0:T(8,128)(2,1)S(1)} collective-permute-done((bf16[4,7,128,128]{3,2,1,0:T(8,128)(2,1)}, bf16[4,7,128,128]{3,2,1,0:T(8,128)(2,1)S(1)}, u32[]{:S(2)}, u32[]{:S(2)}) %collective-permute-start) | collective-permute-done | bytes 917536 | tf_op jit(solution)/shard_map/ppermute | solution.py:115
  79.9 2.7 %add_convert_fusion = bf16[4,7,128,128]{3,2,1,0:T(8,128)(2,1)} fusion(f32[4,7,128,128]{3,2,1,0:T(8,128)} %shard_map.112, bf16[4,7,128,128]{3,2,1,0:T(8,128)(2,1)S(1)} %collective-permute-done), kind=kLoop, calls=%fused_computation.6 | loop fusion | flops 1376256 | bytes 3670016 | tf_op jit(solution)/shard_map/convert_element_type | solution.py:118
  82.6 5.1 %all-to-all-start.2 = ((bf16[4,7,128,128]{3,2,1,0:T(8,128)(2,1)}), bf16[4,7,128,128]{3,2,1,0:T(8,128)(2,1)S(1)}, u32[]{:S(2)}, u32[]{:S(2)}) async-start(bf16[4,7,128,128]{3,2,1,0:T(8,128)(2,1)} %add_convert_fusion), calls=%async_computation.2 | async-start | bytes 1835008 | tf_op jit(solution)/shard_map/all_to_all | solution.py:117
  87.7 0.0 copy-start.6
  87.7 0.0 copy-start.4
  87.7 1.3 %slice.21 = f32[256,1,128]{2,1,0:T(1,128)S(1)} slice(f32[256,27,128]{2,1,0:T(8,128)} %copy-done.1), slice={[0:256], [0:1], [0:128]} | slice | bytes 262144 | tf_op jit(solution)/shard_map/slice | solution.py:35
  89.1 20.4 %all-to-all-done.2 = bf16[4,7,128,128]{3,2,1,0:T(8,128)(2,1)S(1)} async-done(((bf16[4,7,128,128]{3,2,1,0:T(8,128)(2,1)}), bf16[4,7,128,128]{3,2,1,0:T(8,128)(2,1)S(1)}, u32[]{:S(2)}, u32[]{:S(2)}) %all-to-all-start.2) | async-done | bytes 917536 | tf_op jit(solution)/shard_map/all_to_all | solution.py:117
  109.5 0.2 reduce_sum.21
  109.6 0.7 copy.47
  110.3 3.4 %all-to-all-start.3 = ((bf16[4,7,32,128]{3,2,1,0:T(8,128)(2,1)}), bf16[4,7,32,128]{3,2,1,0:T(8,128)(2,1)S(1)}, u32[]{:S(2)}, u32[]{:S(2)}) async-start(bf16[4,7,32,128]{3,2,1,0:T(8,128)(2,1)} %copy.47), calls=%async_computation.3 | async-start | bytes 458752 | tf_op jit(solution)/shard_map/all_to_all | solution.py:127
  113.7 1.9 %fusion.7 = bf16[256,128]{1,0:T(8,128)(2,1)} fusion(f32[256,128]{1,0:T(8,128)S(1)} %bitcast.33, bf16[256,1024]{1,0:T(8,128)(2,1)S(1)} %copy-done, bf16[479,1024]{1,0:T(8,128)(2,1)} %param.12), kind=kOutput, calls=%fused_computation.11 | convolution fusion | flops 67174400 | bytes 983040 | tf_op jit(solution)/shard_map/bh,zh->bz/dot_general | solution.py:28
  115.6 3.7 %all-to-all-done.3 = bf16[4,7,32,128]{3,2,1,0:T(8,128)(2,1)S(1)} async-done(((bf16[4,7,32,128]{3,2,1,0:T(8,128)(2,1)}), bf16[4,7,32,128]{3,2,1,0:T(8,128)(2,1)S(1)}, u32[]{:S(2)}, u32[]{:S(2)}) %all-to-all-start.3) | async-done | bytes 229408 | tf_op jit(solution)/shard_map/all_to_all | solution.py:127
  119.4 0.2 fusion.12
  119.5 0.0 copy-done.6
  119.5 0.6 sqrt_add_fusion
  120.2 0.0 copy-done.4
  120.2 0.9 fusion.11
  (1 shorter events, 0.0 us)
Async XLA Ops:
  0.6 5.7 %copy-start = (bf16[256,1024]{1,0:T(8,128)(2,1)S(1)}, bf16[256,1024]{1,0:T(8,128)(2,1)}, u32[]{:S(2)}) copy-start(bf16[256,1024]{1,0:T(8,128)(2,1)} %param.11) | copy-start | bytes 1572868
  2.1 21.4 %all-to-all-start = ((s32[4,7,256]{2,1,0:T(8,128)}), s32[4,7,256]{2,1,0:T(8,128)S(1)}, u32[]{:S(2)}, u32[]{:S(2)}) async-start(s32[4,7,256]{2,1,0:T(8,128)} %reshape.26), calls=%async_computation | async-start | bytes 65536 | tf_op jit(solution)/shard_map/all_to_all | solution.py:85
  9.2 4.5 %copy-start.3 = (bf16[256,26,128]{2,0,1:T(8,128)(2,1)S(1)}, bf16[256,26,128]{2,0,1:T(8,128)(2,1)}, u32[]{:S(2)}) copy-start(bf16[256,26,128]{2,0,1:T(8,128)(2,1)} %param.9) | copy-start | bytes 5111812
  13.7 1.2 copy-start.5
  19.4 2.0 %copy-start.1 = (f32[256,27,128]{2,1,0:T(8,128)}, f32[256,27,128]{2,1,0:T(8,128)S(1)}, u32[]{:S(2)}) copy-start(f32[256,27,128]{2,1,0:T(8,128)S(1)} %fusion.1) | copy-start | bytes 10616836
  23.5 26.4 %all-to-all-start.1 = ((bf16[4,7,256,128]{3,2,1,0:T(8,128)(2,1)}), bf16[4,7,256,128]{3,2,1,0:T(8,128)(2,1)S(1)}, u32[]{:S(2)}, u32[]{:S(2)}) async-start(bf16[4,7,256,128]{3,2,1,0:T(8,128)(2,1)} %bitcast.29), calls=%async_computation.1 | async-start | bytes 3670016 | tf_op jit(solution)/shard_map/all_to_all | solution.py:91
  49.9 1.2 %copy-start.2 = (bf16[4,7,256,128]{3,2,1,0:T(8,128)(2,1)}, bf16[4,7,256,128]{3,2,1,0:T(8,128)(2,1)S(1)}, u32[]{:S(2)}) copy-start(bf16[4,7,256,128]{3,2,1,0:T(8,128)(2,1)S(1)} %all-to-all-done.1.rows_ref) | copy-start | bytes 5505028
  57.7 22.2 %collective-permute-start = (bf16[4,7,128,128]{3,2,1,0:T(8,128)(2,1)}, bf16[4,7,128,128]{3,2,1,0:T(8,128)(2,1)S(1)}, u32[]{:S(2)}, u32[]{:S(2)}) collective-permute-start(bf16[4,7,128,128]{3,2,1,0:T(8,128)(2,1)} %shard_map.113), channel_id=1, source_target_pairs={{0,4},{4,0},{8,12},{12,8},{16,20},{20,16},{24,28},{28,24},{1,5},{5... | collective-permute-start | bytes 2752520 | tf_op jit(solution)/shard_map/ppermute | solution.py:115
  82.6 26.9 %all-to-all-start.2 = ((bf16[4,7,128,128]{3,2,1,0:T(8,128)(2,1)}), bf16[4,7,128,128]{3,2,1,0:T(8,128)(2,1)S(1)}, u32[]{:S(2)}, u32[]{:S(2)}) async-start(bf16[4,7,128,128]{3,2,1,0:T(8,128)(2,1)} %add_convert_fusion), calls=%async_computation.2 | async-start | bytes 1835008 | tf_op jit(solution)/shard_map/all_to_all | solution.py:117
  87.7 31.8 %copy-start.6 = (f32[26,32]{1,0:T(8,128)S(1)}, f32[26,32]{1,0:T(8,128)}, u32[]{:S(2)}) copy-start(f32[26,32]{1,0:T(8,128)} %param.16) | copy-start | bytes 9988
  87.7 32.5 %copy-start.4 = (f32[26,32,128]{2,1,0:T(8,128)S(1)}, f32[26,32,128]{2,1,0:T(8,128)}, u32[]{:S(2)}) copy-start(f32[26,32,128]{2,1,0:T(8,128)} %param.15) | copy-start | bytes 1277956
  110.3 9.0 %all-to-all-start.3 = ((bf16[4,7,32,128]{3,2,1,0:T(8,128)(2,1)}), bf16[4,7,32,128]{3,2,1,0:T(8,128)(2,1)S(1)}, u32[]{:S(2)}, u32[]{:S(2)}) async-start(bf16[4,7,32,128]{3,2,1,0:T(8,128)(2,1)} %copy.47), calls=%async_computation.3 | async-start | bytes 458752 | tf_op jit(solution)/shard_map/all_to_all | solution.py:127

commit v2 on v1

v2 whole, which is shorter than its diff:
```python
import jax
import jax.numpy as jnp
import numpy as np
from jax import lax
from jax.experimental import pallas as pl
from jax.experimental.pallas import tpu as pltpu
from jax.sharding import PartitionSpec as P

LEARN_RATE = 0.1
EPSILON = 1e-08


def symmetric_rows(feature_count, wanted):
    row_index, col_index = np.tril_indices(feature_count, -1)
    pair_of = np.full((feature_count, feature_count), -1)
    pair_of[row_index, col_index] = np.arange(row_index.shape[0])
    pair_of[col_index, row_index] = np.arange(row_index.shape[0])
    matrix = np.zeros((len(wanted), feature_count, row_index.shape[0]), np.float32)
    for place, i in enumerate(wanted):
        for j in range(feature_count):
            if 0 <= i < feature_count and i != j:
                matrix[place, j, pair_of[i, j]] = 1.0
    return jnp.asarray(matrix.reshape(-1, row_index.shape[0]), jnp.bfloat16)


def feature_grads(features, top_cot, pair_weight, wanted):
    batch_rows, feature_count, _ = features.shape
    expanded = jnp.dot(
        symmetric_rows(feature_count, wanted), pair_weight, preferred_element_type=jnp.float32
    ).astype(jnp.bfloat16)
    symmetric = jnp.einsum("bh,zh->bz", top_cot, expanded, preferred_element_type=jnp.float32)
    symmetric = symmetric.reshape(batch_rows, len(wanted), feature_count)
    return jnp.einsum("bij,bje->bie", symmetric, features, precision=lax.Precision.HIGH)


def sum_kernel(ids_ref, rows_ref, out_ref):
    sources = rows_ref.shape[0]
    blocks, _, block_rows, width = out_ref.shape
    samples = rows_ref.shape[2]
    base = pl.program_id(1) * (blocks * block_rows)
    target = lax.broadcasted_iota(jnp.int32, (blocks * block_rows, samples), 0) + base
    total = jnp.zeros((blocks * block_rows, width), jnp.float32)
    for s in range(sources):
        onehot = (target == ids_ref[s, 0]).astype(jnp.float32).astype(jnp.bfloat16)
        total = total + jnp.dot(onehot, rows_ref[s, 0], preferred_element_type=jnp.float32)
    out_ref[...] = total.reshape(blocks, 1, block_rows, width).astype(out_ref.dtype)


def sum_rows(ids, rows, blocks, block_rows, dtype):
    sources, tables, samples, width = rows.shape
    step = 4 if blocks % 4 == 0 else 1
    return pl.pallas_call(
        sum_kernel,
        grid=(tables, blocks // step),
        in_specs=[
            pl.BlockSpec((sources, 1, 1, samples), lambda t, h: (0, t, 0, 0)),
            pl.BlockSpec((sources, 1, samples, width), lambda t, h: (0, t, 0, 0)),
        ],
        out_specs=pl.BlockSpec((step, 1, block_rows, width), lambda t, h: (h, t, 0, 0)),
        out_shape=jax.ShapeDtypeStruct((blocks, tables, block_rows, width), dtype),
        cost_estimate=pl.CostEstimate(
            flops=2 * tables * sources * samples * blocks * block_rows * width,
            bytes_accessed=rows.size * 2 + blocks * tables * block_rows * width * 4,
            transcendentals=0,
        ),
    )(ids[:, :, None, :], rows)


def per_device(sparse_vecs, dense_vec, top_cot, top_weight, owner_ids, local_rows, table, accum):
    batch_rows, table_count, row_width = sparse_vecs.shape
    dp_count, mp_count = lax.axis_size("dp"), lax.axis_size("mp")
    rows_own = table.shape[1]
    group_rows = rows_own * mp_count
    per_mp = -(-table_count // mp_count)
    padding = per_mp * mp_count - table_count
    inner = 2 if dp_count % 2 == 0 else 1
    outer = dp_count // inner
    first = (per_mp + 1) // 2
    chunks = [range(first), range(first, per_mp)]

    keys = (owner_ids[:, :, 0] * group_rows + local_rows).T
    keys = jnp.pad(keys, ((0, padding), (0, 0)), constant_values=-1)
    keys = keys.reshape(per_mp, mp_count, batch_rows).transpose(1, 0, 2)
    keys = lax.all_to_all(keys, "mp", split_axis=0, concat_axis=0, tiled=True)
    owner, local = keys // group_rows, keys % group_rows
    place = owner // inner * group_rows + local
    part = owner % inner
    mine = lax.axis_index("dp") % inner
    own_place = jnp.where((keys >= 0) & (part == mine), place, -1)
    other_place = jnp.where((keys >= 0) & (part != mine), place, -1)

    features = jnp.concatenate([dense_vec[:, None, :], sparse_vecs], axis=1).astype(jnp.float32)
    pair_weight = top_weight[row_width:]
    swap = [(i, i ^ 1) for i in range(dp_count)]
    groups = [[r + inner * k for k in range(outer)] for r in range(inner)]
    sums = []
    for chunk in chunks:
        wanted = [1 + k * mp_count + m for m in range(mp_count) for k in chunk]
        last = chunk is chunks[-1]
        grads = feature_grads(features, top_cot, pair_weight, wanted + [0] if last else wanted)
        if last:
            direct = jnp.einsum(
                "bh,zh->bz", top_cot, top_weight[:row_width], preferred_element_type=jnp.float32
            )
            dense_grad = (direct + grads[:, -1]).astype(jnp.bfloat16)
            grads = grads[:, :-1]
        send = grads.astype(jnp.bfloat16).transpose(1, 0, 2)
        rows = lax.all_to_all(
            send.reshape(mp_count, len(chunk), batch_rows, row_width),
            "mp",
            split_axis=0,
            concat_axis=0,
            tiled=True,
        )
        cut = slice(chunk[0], chunk[-1] + 1)
        total = sum_rows(own_place[:, cut], rows, outer, group_rows, jnp.float32)
        if inner == 2:
            other = sum_rows(other_place[:, cut], rows, outer, group_rows, jnp.bfloat16)
            total = total + lax.ppermute(other, "dp", swap).astype(jnp.float32)
        parts = lax.all_to_all(
            total.astype(jnp.bfloat16),
            "dp",
            split_axis=0,
            concat_axis=0,
            axis_index_groups=groups,
            tiled=True,
        )
        sums.append(jnp.sum(parts.astype(jnp.float32), axis=0).astype(jnp.bfloat16))
    summed = jnp.concatenate(sums, axis=0)
    summed = summed.reshape(per_mp, mp_count, rows_own, row_width).transpose(1, 0, 2, 3)
    row_grad = lax.all_to_all(summed, "mp", split_axis=0, concat_axis=0, tiled=True)
    row_grad = row_grad.transpose(1, 0, 2, 3).reshape(per_mp * mp_count, rows_own, row_width)
    row_grad = row_grad[:table_count].astype(jnp.float32)
    new_accum = accum + jnp.mean(row_grad * row_grad, axis=-1)
    new_table = table - LEARN_RATE * row_grad / (jnp.sqrt(new_accum)[:, :, None] + EPSILON)
    return (dense_grad, new_table, new_accum)


def solution(mesh):
    in_specs = (
        P(("dp", "mp"), None, None),
        P(("dp", "mp"), None),
        P(("dp", "mp"), None),
        P(),
        P(("dp", "mp"), None, None),
        P(("dp", "mp"), None),
        P(None, ("dp", "mp"), None),
        P(None, ("dp", "mp")),
    )
    out_specs = (P(("dp", "mp"), None), P(None, ("dp", "mp"), None), P(None, ("dp", "mp")))
    return jax.shard_map(
        per_device, mesh=mesh, in_specs=in_specs, out_specs=out_specs, check_vma=False
    )
```

time: 122 us -> 107 us (0.88)
  waiting for transfers between devices: 59.1 us -> 21.8 us
  starting transfers between devices: 18.3 us -> 27.8 us
  local copies, waits for them, and re-layouts: 15.1 us -> 20.8 us
  Pallas kernels: 13.2 us -> 15.6 us
  matrix products: 9.1 us -> 11.4 us
  other arithmetic: 5.53 us -> 7.41 us
    all_to_all x2 -> x3, waiting for transfers between devices: 22.1 us -> 1.47 us  [the longest x2 1.46 us: per_device(): lax.all_to_all(send.reshape(mp_count, len(chunk), batch_rows, row_width),...]
    ppermute x1 -> x2, waiting for transfers between devices: 12.9 us -> 1.23 us  [per_device(): total = total + lax.ppermute(other, 'dp', swap).astype(jnp.float32)]
    all_to_all x1 -> x2, waiting for transfers between devices: 20.4 us -> 15.4 us  [per_device(): lax.all_to_all(total.astype(jnp.bfloat16), 'dp', split_axis=0, concat_axi...]
    all_to_all x2 -> x3, starting transfers between devices: 7.85 us -> 11.7 us  [the longest x2 7.4 us: per_device(): lax.all_to_all(send.reshape(mp_count, len(chunk), batch_rows, row_width),...]
    reshape x3 -> x6, local copies, waits for them, and re-layouts: 5.18 us -> 8.55 us  [the longest x4 7.91 us: feature_grads(): symmetric = symmetric.reshape(batch_rows, len(wanted), feature_count)]
    all_to_all x1 -> x2, starting transfers between devices: 5.12 us -> 8.34 us  [per_device(): lax.all_to_all(total.astype(jnp.bfloat16), 'dp', split_axis=0, concat_axi...]
    ppermute x1 -> x2, starting transfers between devices: 1.99 us -> 4.43 us  [per_device(): total = total + lax.ppermute(other, 'dp', swap).astype(jnp.float32)]
    pallas_call x2 -> x4, Pallas kernels: 13.2 us -> 15.6 us  [sum_rows(): pl.pallas_call(sum_kernel, grid=(tables, blocks // step), in_specs=[pl.Bl...]
  transfers between devices with their start and end apart: 5 -> 8, of which waited for: 4 -> 5; matrix products, arithmetic and copies ran while one was open for 17% -> 31% of each run, Pallas kernels for 6% -> 15%
where the time goes in v2:
time: 107 us; the launch traced here: 106 us
  starting transfers between devices  27.8 us (26%)
  waiting for transfers between devices  21.8 us (20%)
  local copies, waits for them, and re-layouts  20.8 us (19%)
  Pallas kernels  15.6 us (15%)
  matrix products  11.4 us (11%)
  other arithmetic  7.41 us (7%)
    pallas_call x4, Pallas kernels, sum_rows(): pl.pallas_call(sum_kernel, grid=(tables, blocks // step), in_specs=[pl.Bl...  15.6 us
    all_to_all x2, waiting for transfers between devices, per_device(): lax.all_to_all(total.astype(jnp.bfloat16), 'dp', split_axis=0, concat_axi...  15.4 us
    all_to_all x2, starting transfers between devices, per_device(): lax.all_to_all(total.astype(jnp.bfloat16), 'dp', split_axis=0, concat_axi...  8.34 us
    reshape x4, local copies, waits for them, and re-layouts, feature_grads(): symmetric = symmetric.reshape(batch_rows, len(wanted), feature_count)  7.91 us
    all_to_all x2, starting transfers between devices, per_device(): lax.all_to_all(send.reshape(mp_count, len(chunk), batch_rows, row_width),...  7.4 us
    unnamed x19, local copies, waits for them, and re-layouts  5.07 us
    dot_general x2, matrix products, feature_grads(): jnp.einsum('bh,zh->bz', top_cot, expanded, preferred_element_type=jnp.flo...  4.95 us
    dot_general x2, matrix products, feature_grads(): jnp.einsum('bij,bje->bie', symmetric, features, precision=lax.Precision.H...  4.58 us
  transfers between devices with their start and end apart: 8, of which 5 were waited for; matrix products, arithmetic and copies ran while one was open for 31% of the time, Pallas kernels for 15%

profile of v2, /device:TPU:0, one launch (start us, length us, event | category | flops | bytes accessed | tf_op | source)
XLA Modules:
  0.0 105.6 jit_solution(14211095092033941270)
XLA Ops:
  0.6 0.0 copy-start
  0.6 0.8 fusion.18
  1.5 0.6 copy.89
  2.1 4.3 %all-to-all-start = ((s32[4,7,256]{2,1,0:T(8,128)}), s32[4,7,256]{2,1,0:T(8,128)}, u32[]{:S(2)}, u32[]{:S(2)}) async-start(s32[4,7,256]{2,1,0:T(8,128)} %bitcast.45), calls=%async_computation | async-start | bytes 65536 | tf_op jit(solution)/shard_map/all_to_all | solution.py:84
  6.4 0.0 copy-done
  6.4 2.0 %fusion.5 = f32[256,351]{0,1:T(8,128)S(1)} fusion(bf16[256,1024]{1,0:T(8,128)(2,1)S(1)} %copy-done, bf16[351,351]{1,0:T(8,128)(2,1)} %constant.79.clone, bf16[479,1024]{1,0:T(8,128)(2,1)} %param.13), kind=kOutput, calls=%fused_computation.10 | convolution fusion | flops 436700160 | bytes 1874944 | tf_op jit(solution)/shard_map/bh,zh->bz/dot_general | solution.py:31
  8.5 2.5 %copy.66 = f32[256,13,27]{2,1,0:T(8,128)} copy(f32[256,13,27]{0,2,1:T(8,128)S(1)} %reshape.31) | data formatting | bytes 718848 | tf_op jit(solution)/shard_map/reshape | solution.py:32
  11.0 0.0 copy-start.7
  11.0 2.7 %copy.65 = bf16[256,26,128]{2,1,0:T(8,128)(2,1)S(1)} copy(bf16[256,26,128]{2,0,1:T(8,128)(2,1)} %param.10) | data formatting | bytes 3407872 | tf_op args[0]
  13.7 0.0 copy-done.7
  13.7 0.1 copy.64
  13.8 0.0 copy-done.1
  13.8 1.5 %fusion.2 = f32[256,13,128]{2,1,0:T(8,128)S(1)} fusion(f32[256,13,27]{2,1,0:T(8,128)S(1)} %copy-done.1, bf16[256,26,128]{2,1,0:T(8,128)(2,1)S(1)} %copy.65, bf16[256,1,128]{2,1,0:T(2,128)(2,1)S(1)} %copy.64), kind=kOutput, calls=%fused_computation.7 | convolution fusion | flops 72548352 | bytes 3832832 | tf_op jit(solution)/shard_map/bij,bje->bie/dot_general | solution.py:33
  15.3 0.0 copy-start.2
  15.4 1.3 %copy-done.2 = f32[256,13,128]{2,1,0:T(8,128)} copy-done((f32[256,13,128]{2,1,0:T(8,128)}, f32[256,13,128]{2,1,0:T(8,128)S(1)}, u32[]{:S(2)}) %copy-start.2) | copy-done | bytes 1703960
  16.7 0.1 fusion.7
  16.8 1.1 %copy.74 = bf16[12,256,128]{2,1,0:T(8,128)(2,1)} copy(bf16[12,256,128]{2,0,1:T(8,128)(2,1)S(1)} %fusion.7) | data formatting | bytes 1572864 | tf_op jit(solution)/shard_map/transpose | solution.py:107
  17.9 0.0 all-to-all-done
  17.9 3.9 %all-to-all-start.3 = ((bf16[4,3,256,128]{3,2,1,0:T(8,128)(2,1)}), bf16[4,3,256,128]{3,2,1,0:T(8,128)(2,1)S(1)}, u32[]{:S(2)}, u32[]{:S(2)}) async-start(bf16[4,3,256,128]{3,2,1,0:T(8,128)(2,1)} %bitcast.12), calls=%async_computation.3 | async-start | bytes 1572864 | tf_op jit(solution)/shard_map/all_to_all | solution.py:108
  21.8 2.9 %fusion.4 = f32[256,432]{0,1:T(8,128)} fusion(bf16[256,1024]{1,0:T(8,128)(2,1)S(1)} %copy-done, bf16[432,351]{1,0:T(8,128)(2,1)} %constant.78.clone, bf16[479,1024]{1,0:T(8,128)(2,1)} %param.13), kind=kOutput, calls=%fused_computation.9 | convolution fusion | flops 537477120 | bytes 2019328 | tf_op jit(solution)/shard_map/bh,zh->bz/dot_general | solution.py:31
  24.7 1.9 %reshape.33 = f32[256,16,27]{0,2,1:T(8,128)} reshape(f32[256,432]{0,1:T(8,128)} %fusion.4) | data formatting | bytes 884736 | tf_op jit(solution)/shard_map/reshape | solution.py:32
  26.6 3.5 %copy.70 = f32[256,16,27]{2,1,0:T(8,128)} copy(f32[256,16,27]{0,2,1:T(8,128)} %reshape.33) | data formatting | bytes 884736 | tf_op jit(solution)/shard_map/reshape | solution.py:32
  30.1 3.1 %fusion = bf16[16,256,128]{2,0,1:T(8,128)(2,1)S(1)} fusion(f32[256,16,27]{2,1,0:T(8,128)} %copy.70, bf16[256,26,128]{2,1,0:T(8,128)(2,1)S(1)} %copy.65, bf16[256,1,128]{2,1,0:T(2,128)(2,1)S(1)} %copy.64), kind=kOutput, calls=%fused_computation.5 | convolution fusion | flops 88997888 | bytes 3260416 | tf_op jit(solution)/shard_map/bij,bje->bie/dot_general | solution.py:33
  33.2 1.2 %copy.71 = bf16[16,256,128]{2,1,0:T(8,128)(2,1)} copy(bf16[16,256,128]{2,0,1:T(8,128)(2,1)S(1)} %fusion) | data formatting | bytes 2097152 | tf_op jit(solution)/shard_map/convert_element_type | solution.py:107
  34.4 0.0 all-to-all-done.3.rows_ref
  34.4 3.5 %all-to-all-start.1 = ((bf16[4,4,256,128]{3,2,1,0:T(8,128)(2,1)}), bf16[4,4,256,128]{3,2,1,0:T(8,128)(2,1)S(1)}, u32[]{:S(2)}, u32[]{:S(2)}) async-start(bf16[4,4,256,128]{3,2,1,0:T(8,128)(2,1)} %bitcast.9), calls=%async_computation.1 | async-start | bytes 2097152 | tf_op jit(solution)/shard_map/all_to_all | solution.py:108
  38.0 0.8 and_select_fusion
  38.8 0.6 copy.77.ids_ref
  39.4 0.0 copy-done.4
  39.4 3.5 %shard_map.124 = bf16[4,3,128,128]{3,2,1,0:T(8,128)(2,1)} custom-call(s32[4,3,1,256]{3,2,1,0:T(1,128)} %copy.77.ids_ref, bf16[4,3,256,128]{3,2,1,0:T(8,128)(2,1)} %copy-done.4), custom_call_target="tpu_custom_call" | custom-call | flops 402653184 | bytes 1572864 | tf_op jit(solution)/shard_map/pallas_call | solution.py:52
  43.0 2.2 %collective-permute-start.1 = (bf16[4,3,128,128]{3,2,1,0:T(8,128)(2,1)}, bf16[4,3,128,128]{3,2,1,0:T(8,128)(2,1)S(1)}, u32[]{:S(2)}, u32[]{:S(2)}) collective-permute-start(bf16[4,3,128,128]{3,2,1,0:T(8,128)(2,1)} %shard_map.124), channel_id=1, source_target_pairs={{0,4},{4,0},{8,12},{12,8},{16,20},{20,16},{24,28},{28,24},{1,5},{5... | collective-permute-start | bytes 1179656 | tf_op jit(solution)/shard_map/ppermute | solution.py:119
  45.2 0.8 and_select_fusion.1
  46.0 0.6 copy.75.ids_ref
  46.6 0.6 broadcast_in_dim.21.ids_ref
  47.3 3.6 %shard_map.123 = f32[4,3,128,128]{3,2,1,0:T(8,128)} custom-call(s32[4,3,1,256]{3,2,1,0:T(1,128)} %copy.75.ids_ref, bf16[4,3,256,128]{3,2,1,0:T(8,128)(2,1)} %copy-done.4), custom_call_target="tpu_custom_call" | custom-call | flops 402653184 | bytes 1572864 | tf_op jit(solution)/shard_map/pallas_call | solution.py:52
  50.9 1.5 %all-to-all-done.1.rows_ref = bf16[4,4,256,128]{3,2,1,0:T(8,128)(2,1)S(1)} async-done(((bf16[4,4,256,128]{3,2,1,0:T(8,128)(2,1)}), bf16[4,4,256,128]{3,2,1,0:T(8,128)(2,1)S(1)}, u32[]{:S(2)}, u32[]{:S(2)}) %all-to-all-start.1) | async-done | bytes 1048608 | tf_op jit(solution)/shard_map/all_to_all | solution.py:108
  52.4 1.0 copy-done.3
  53.3 4.2 %shard_map.122 = bf16[4,4,128,128]{3,2,1,0:T(8,128)(2,1)} custom-call(s32[4,4,1,256]{3,2,1,0:T(1,128)} %broadcast_in_dim.21.ids_ref, bf16[4,4,256,128]{3,2,1,0:T(8,128)(2,1)} %copy-done.3), custom_call_target="tpu_custom_call" | custom-call | flops 536870912 | bytes 2097152 | tf_op jit(solution)/shard_map/pallas_call | solution.py:52
  57.5 2.2 %collective-permute-start = (bf16[4,4,128,128]{3,2,1,0:T(8,128)(2,1)}, bf16[4,4,128,128]{3,2,1,0:T(8,128)(2,1)S(1)}, u32[]{:S(2)}, u32[]{:S(2)}) collective-permute-start(bf16[4,4,128,128]{3,2,1,0:T(8,128)(2,1)} %shard_map.122), channel_id=1, source_target_pairs={{0,4},{4,0},{8,12},{12,8},{16,20},{20,16},{24,28},{28,24},{1,5},{5... | collective-permute-start | bytes 1572872 | tf_op jit(solution)/shard_map/ppermute | solution.py:119
  59.7 0.0 collective-permute-done.1
  59.7 0.0 copy-done.5
  59.7 0.8 add_convert_fusion.1
  60.6 4.9 %all-to-all-start.4 = ((bf16[4,3,128,128]{3,2,1,0:T(8,128)(2,1)}), bf16[4,3,128,128]{3,2,1,0:T(8,128)(2,1)S(1)}, u32[]{:S(2)}, u32[]{:S(2)}) async-start(bf16[4,3,128,128]{3,2,1,0:T(8,128)(2,1)} %add_convert_fusion.1), calls=%async_computation.4 | async-start | bytes 786432 | tf_op jit(solution)/shard_map/all_to_all | solution.py:120
  65.4 0.6 copy.72.ids_ref
  66.1 4.3 %shard_map.121 = f32[4,4,128,128]{3,2,1,0:T(8,128)} custom-call(s32[4,4,1,256]{3,2,1,0:T(1,128)} %copy.72.ids_ref, bf16[4,4,256,128]{3,2,1,0:T(8,128)(2,1)} %copy-done.3), custom_call_target="tpu_custom_call" | custom-call | flops 536870912 | bytes 2097152 | tf_op jit(solution)/shard_map/pallas_call | solution.py:52
  70.3 1.2 %collective-permute-done = bf16[4,4,128,128]{3,2,1,0:T(8,128)(2,1)S(1)} collective-permute-done((bf16[4,4,128,128]{3,2,1,0:T(8,128)(2,1)}, bf16[4,4,128,128]{3,2,1,0:T(8,128)(2,1)S(1)}, u32[]{:S(2)}, u32[]{:S(2)}) %collective-permute-start) | collective-permute-done | bytes 524320 | tf_op jit(solution)/shard_map/ppermute | solution.py:119
  71.5 2.2 %add_convert_fusion = bf16[4,4,128,128]{3,2,1,0:T(8,128)(2,1)} fusion(f32[4,4,128,128]{3,2,1,0:T(8,128)} %shard_map.121, bf16[4,4,128,128]{3,2,1,0:T(8,128)(2,1)S(1)} %collective-permute-done), kind=kLoop, calls=%fused_computation.14 | loop fusion | flops 786432 | bytes 2097152 | tf_op jit(solution)/shard_map/convert_element_type | solution.py:121
  73.7 2.8 %all-to-all-done.4 = bf16[4,3,128,128]{3,2,1,0:T(8,128)(2,1)S(1)} async-done(((bf16[4,3,128,128]{3,2,1,0:T(8,128)(2,1)}), bf16[4,3,128,128]{3,2,1,0:T(8,128)(2,1)S(1)}, u32[]{:S(2)}, u32[]{:S(2)}) %all-to-all-start.4) | async-done | bytes 393248 | tf_op jit(solution)/shard_map/all_to_all | solution.py:120
  76.5 3.5 %all-to-all-start.2 = ((bf16[4,4,128,128]{3,2,1,0:T(8,128)(2,1)}), bf16[4,4,128,128]{3,2,1,0:T(8,128)(2,1)S(1)}, u32[]{:S(2)}, u32[]{:S(2)}) async-start(bf16[4,4,128,128]{3,2,1,0:T(8,128)(2,1)} %add_convert_fusion), calls=%async_computation.2 | async-start | bytes 1048576 | tf_op jit(solution)/shard_map/all_to_all | solution.py:120
  80.0 1.3 %slice.37 = f32[256,1,128]{2,1,0:T(1,128)S(1)} slice(f32[256,13,128]{2,1,0:T(8,128)} %copy-done.2), slice={[0:256], [12:13], [0:128]} | slice | bytes 262144 | tf_op jit(solution)/shard_map/slice | solution.py:105
  81.4 0.0 copy-start.8
  81.4 0.0 copy-start.6
  81.4 0.1 reduce_sum.34
  81.5 12.6 %all-to-all-done.2 = bf16[4,4,128,128]{3,2,1,0:T(8,128)(2,1)S(1)} async-done(((bf16[4,4,128,128]{3,2,1,0:T(8,128)(2,1)}), bf16[4,4,128,128]{3,2,1,0:T(8,128)(2,1)S(1)}, u32[]{:S(2)}, u32[]{:S(2)}) %all-to-all-start.2) | async-done | bytes 524320 | tf_op jit(solution)/shard_map/all_to_all | solution.py:120
  94.0 0.1 reduce_sum.33
  94.2 0.7 copy.78
  94.9 3.4 %all-to-all-start.5 = ((bf16[4,7,32,128]{3,2,1,0:T(8,128)(2,1)}), bf16[4,7,32,128]{3,2,1,0:T(8,128)(2,1)S(1)}, u32[]{:S(2)}, u32[]{:S(2)}) async-start(bf16[4,7,32,128]{3,2,1,0:T(8,128)(2,1)} %copy.78), calls=%async_computation.5 | async-start | bytes 458752 | tf_op jit(solution)/shard_map/all_to_all | solution.py:131
  98.3 1.9 %fusion.6 = bf16[256,128]{1,0:T(8,128)(2,1)} fusion(f32[256,128]{1,0:T(8,128)S(1)} %bitcast.49, bf16[256,1024]{1,0:T(8,128)(2,1)S(1)} %copy-done, bf16[479,1024]{1,0:T(8,128)(2,1)} %param.13), kind=kOutput, calls=%fused_computation.12 | convolution fusion | flops 67174400 | bytes 983040 | tf_op jit(solution)/shard_map/bh,zh->bz/dot_general | solution.py:102
  100.1 3.7 %all-to-all-done.5 = bf16[4,7,32,128]{3,2,1,0:T(8,128)(2,1)S(1)} async-done(((bf16[4,7,32,128]{3,2,1,0:T(8,128)(2,1)}), bf16[4,7,32,128]{3,2,1,0:T(8,128)(2,1)S(1)}, u32[]{:S(2)}, u32[]{:S(2)}) %all-to-all-start.5) | async-done | bytes 229408 | tf_op jit(solution)/shard_map/all_to_all | solution.py:131
  103.9 0.2 fusion.14
  104.1 0.0 copy-done.8
  104.1 0.6 sqrt_add_fusion
  104.7 0.0 copy-done.6
  104.7 0.9 fusion.13
  (13 shorter events, 0.1 us)
Async XLA Ops:
  0.6 5.8 %copy-start = (bf16[256,1024]{1,0:T(8,128)(2,1)S(1)}, bf16[256,1024]{1,0:T(8,128)(2,1)}, u32[]{:S(2)}) copy-start(bf16[256,1024]{1,0:T(8,128)(2,1)} %param.12) | copy-start | bytes 1572868
  2.1 15.8 %all-to-all-start = ((s32[4,7,256]{2,1,0:T(8,128)}), s32[4,7,256]{2,1,0:T(8,128)}, u32[]{:S(2)}, u32[]{:S(2)}) async-start(s32[4,7,256]{2,1,0:T(8,128)} %bitcast.45), calls=%async_computation | async-start | bytes 65536 | tf_op jit(solution)/shard_map/all_to_all | solution.py:84
  11.0 2.8 %copy-start.7 = (bf16[256,128]{1,0:T(8,128)(2,1)S(1)}, bf16[256,128]{1,0:T(8,128)(2,1)}, u32[]{:S(2)}) copy-start(bf16[256,128]{1,0:T(8,128)(2,1)} %param.11) | copy-start | bytes 196612
  11.0 2.9 %copy-start.1 = (f32[256,13,27]{2,1,0:T(8,128)S(1)}, f32[256,13,27]{2,1,0:T(8,128)}, u32[]{:S(2)}) copy-start(f32[256,13,27]{2,1,0:T(8,128)} %copy.66) | copy-start | bytes 1078276
  15.3 1.3 %copy-start.2 = (f32[256,13,128]{2,1,0:T(8,128)}, f32[256,13,128]{2,1,0:T(8,128)S(1)}, u32[]{:S(2)}) copy-start(f32[256,13,128]{2,1,0:T(8,128)S(1)} %fusion.2) | copy-start | bytes 5111812
  17.9 16.5 %all-to-all-start.3 = ((bf16[4,3,256,128]{3,2,1,0:T(8,128)(2,1)}), bf16[4,3,256,128]{3,2,1,0:T(8,128)(2,1)S(1)}, u32[]{:S(2)}, u32[]{:S(2)}) async-start(bf16[4,3,256,128]{3,2,1,0:T(8,128)(2,1)} %bitcast.12), calls=%async_computation.3 | async-start | bytes 1572864 | tf_op jit(solution)/shard_map/all_to_all | solution.py:108
  34.4 5.0 %copy-start.4 = (bf16[4,3,256,128]{3,2,1,0:T(8,128)(2,1)}, bf16[4,3,256,128]{3,2,1,0:T(8,128)(2,1)S(1)}, u32[]{:S(2)}) copy-start(bf16[4,3,256,128]{3,2,1,0:T(8,128)(2,1)S(1)} %all-to-all-done.3.rows_ref) | copy-start | bytes 2359300
  34.4 17.9 %all-to-all-start.1 = ((bf16[4,4,256,128]{3,2,1,0:T(8,128)(2,1)}), bf16[4,4,256,128]{3,2,1,0:T(8,128)(2,1)S(1)}, u32[]{:S(2)}, u32[]{:S(2)}) async-start(bf16[4,4,256,128]{3,2,1,0:T(8,128)(2,1)} %bitcast.9), calls=%async_computation.1 | async-start | bytes 2097152 | tf_op jit(solution)/shard_map/all_to_all | solution.py:108
  43.0 16.8 %collective-permute-start.1 = (bf16[4,3,128,128]{3,2,1,0:T(8,128)(2,1)}, bf16[4,3,128,128]{3,2,1,0:T(8,128)(2,1)S(1)}, u32[]{:S(2)}, u32[]{:S(2)}) collective-permute-start(bf16[4,3,128,128]{3,2,1,0:T(8,128)(2,1)} %shard_map.124), channel_id=1, source_target_pairs={{0,4},{4,0},{8,12},{12,8},{16,20},{20,16},{24,28},{28,24},{1,5},{5... | collective-permute-start | bytes 1179656 | tf_op jit(solution)/shard_map/ppermute | solution.py:119
  50.9 8.8 %copy-start.5 = (f32[4,3,128,128]{3,2,1,0:T(8,128)S(1)}, f32[4,3,128,128]{3,2,1,0:T(8,128)}, u32[]{:S(2)}) copy-start(f32[4,3,128,128]{3,2,1,0:T(8,128)} %shard_map.123) | copy-start | bytes 2359300
  52.4 1.0 copy-start.3
  57.5 14.0 %collective-permute-start = (bf16[4,4,128,128]{3,2,1,0:T(8,128)(2,1)}, bf16[4,4,128,128]{3,2,1,0:T(8,128)(2,1)S(1)}, u32[]{:S(2)}, u32[]{:S(2)}) collective-permute-start(bf16[4,4,128,128]{3,2,1,0:T(8,128)(2,1)} %shard_map.122), channel_id=1, source_target_pairs={{0,4},{4,0},{8,12},{12,8},{16,20},{20,16},{24,28},{28,24},{1,5},{5... | collective-permute-start | bytes 1572872 | tf_op jit(solution)/shard_map/ppermute | solution.py:119
  60.6 16.0 %all-to-all-start.4 = ((bf16[4,3,128,128]{3,2,1,0:T(8,128)(2,1)}), bf16[4,3,128,128]{3,2,1,0:T(8,128)(2,1)S(1)}, u32[]{:S(2)}, u32[]{:S(2)}) async-start(bf16[4,3,128,128]{3,2,1,0:T(8,128)(2,1)} %add_convert_fusion.1), calls=%async_computation.4 | async-start | bytes 786432 | tf_op jit(solution)/shard_map/all_to_all | solution.py:120
  76.5 17.5 %all-to-all-start.2 = ((bf16[4,4,128,128]{3,2,1,0:T(8,128)(2,1)}), bf16[4,4,128,128]{3,2,1,0:T(8,128)(2,1)S(1)}, u32[]{:S(2)}, u32[]{:S(2)}) async-start(bf16[4,4,128,128]{3,2,1,0:T(8,128)(2,1)} %add_convert_fusion), calls=%async_computation.2 | async-start | bytes 1048576 | tf_op jit(solution)/shard_map/all_to_all | solution.py:120
  81.4 22.7 %copy-start.8 = (f32[26,32]{1,0:T(8,128)S(1)}, f32[26,32]{1,0:T(8,128)}, u32[]{:S(2)}) copy-start(f32[26,32]{1,0:T(8,128)} %param.17) | copy-start | bytes 9988
  81.4 23.3 %copy-start.6 = (f32[26,32,128]{2,1,0:T(8,128)S(1)}, f32[26,32,128]{2,1,0:T(8,128)}, u32[]{:S(2)}) copy-start(f32[26,32,128]{2,1,0:T(8,128)} %param.16) | copy-start | bytes 1277956
  94.9 9.0 %all-to-all-start.5 = ((bf16[4,7,32,128]{3,2,1,0:T(8,128)(2,1)}), bf16[4,7,32,128]{3,2,1,0:T(8,128)(2,1)S(1)}, u32[]{:S(2)}, u32[]{:S(2)}) async-start(bf16[4,7,32,128]{3,2,1,0:T(8,128)(2,1)} %copy.78), calls=%async_computation.5 | async-start | bytes 458752 | tf_op jit(solution)/shard_map/all_to_all | solution.py:131

commit v3 on v2

--- a/solution.py
+++ b/solution.py
@@ -35,7 +35,8 @@
 
 def sum_kernel(ids_ref, rows_ref, out_ref):
     sources = rows_ref.shape[0]
-    blocks, _, block_rows, width = out_ref.shape
+    blocks, shares, _, share_rows, width = out_ref.shape
+    block_rows = shares * share_rows
     samples = rows_ref.shape[2]
     base = pl.program_id(1) * (blocks * block_rows)
     target = lax.broadcasted_iota(jnp.int32, (blocks * block_rows, samples), 0) + base
@@ -43,10 +44,10 @@
     for s in range(sources):
         onehot = (target == ids_ref[s, 0]).astype(jnp.float32).astype(jnp.bfloat16)
         total = total + jnp.dot(onehot, rows_ref[s, 0], preferred_element_type=jnp.float32)
-    out_ref[...] = total.reshape(blocks, 1, block_rows, width).astype(out_ref.dtype)
+    out_ref[...] = total.reshape(out_ref.shape).astype(out_ref.dtype)
 
 
-def sum_rows(ids, rows, blocks, block_rows, dtype):
+def sum_rows(ids, rows, blocks, shares, share_rows, dtype):
     sources, tables, samples, width = rows.shape
     step = 4 if blocks % 4 == 0 else 1
     return pl.pallas_call(
@@ -56,11 +57,13 @@
             pl.BlockSpec((sources, 1, 1, samples), lambda t, h: (0, t, 0, 0)),
             pl.BlockSpec((sources, 1, samples, width), lambda t, h: (0, t, 0, 0)),
         ],
-        out_specs=pl.BlockSpec((step, 1, block_rows, width), lambda t, h: (h, t, 0, 0)),
-        out_shape=jax.ShapeDtypeStruct((blocks, tables, block_rows, width), dtype),
+        out_specs=pl.BlockSpec(
+            (step, shares, 1, share_rows, width), lambda t, h: (h, 0, t, 0, 0)
+        ),
+        out_shape=jax.ShapeDtypeStruct((blocks, shares, tables, share_rows, width), dtype),
         cost_estimate=pl.CostEstimate(
-            flops=2 * tables * sources * samples * blocks * block_rows * width,
-            bytes_accessed=rows.size * 2 + blocks * tables * block_rows * width * 4,
+            flops=2 * tables * sources * samples * blocks * shares * share_rows * width,
+            bytes_accessed=rows.size * 2 + blocks * shares * tables * share_rows * width * 4,
             transcendentals=0,
         ),
     )(ids[:, :, None, :], rows)
@@ -92,7 +95,10 @@
     features = jnp.concatenate([dense_vec[:, None, :], sparse_vecs], axis=1).astype(jnp.float32)
     pair_weight = top_weight[row_width:]
     swap = [(i, i ^ 1) for i in range(dp_count)]
-    groups = [[r + inner * k for k in range(outer)] for r in range(inner)]
+    groups = [
+        [(r + inner * k) * mp_count + m for k in range(outer) for m in range(mp_count)]
+        for r in range(inner)
+    ]
     sums = []
     for chunk in chunks:
         wanted = [1 + k * mp_count + m for m in range(mp_count) for k in chunk]
@@ -113,24 +119,24 @@
             tiled=True,
         )
         cut = slice(chunk[0], chunk[-1] + 1)
-        total = sum_rows(own_place[:, cut], rows, outer, group_rows, jnp.float32)
+        total = sum_rows(own_place[:, cut], rows, outer, mp_count, rows_own, jnp.float32)
         if inner == 2:
-            other = sum_rows(other_place[:, cut], rows, outer, group_rows, jnp.bfloat16)
+            other = sum_rows(other_place[:, cut], rows, outer, mp_count, rows_own, jnp.bfloat16)
             total = total + lax.ppermute(other, "dp", swap).astype(jnp.float32)
         parts = lax.all_to_all(
-            total.astype(jnp.bfloat16),
-            "dp",
+            total.astype(jnp.bfloat16).reshape(
+                outer * mp_count, len(chunk), rows_own, row_width
+            ),
+            ("dp", "mp"),
             split_axis=0,
             concat_axis=0,
             axis_index_groups=groups,
             tiled=True,
         )
-        sums.append(jnp.sum(parts.astype(jnp.float32), axis=0).astype(jnp.bfloat16))
-    summed = jnp.concatenate(sums, axis=0)
-    summed = summed.reshape(per_mp, mp_count, rows_own, row_width).transpose(1, 0, 2, 3)
-    row_grad = lax.all_to_all(summed, "mp", split_axis=0, concat_axis=0, tiled=True)
-    row_grad = row_grad.transpose(1, 0, 2, 3).reshape(per_mp * mp_count, rows_own, row_width)
-    row_grad = row_grad[:table_count].astype(jnp.float32)
+        parts = parts.reshape(outer, mp_count, len(chunk), rows_own, row_width)
+        summed = jnp.sum(parts.astype(jnp.float32), axis=0).transpose(1, 0, 2, 3)
+        sums.append(summed.reshape(len(chunk) * mp_count, rows_own, row_width))
+    row_grad = jnp.concatenate(sums, axis=0)[:table_count]
     new_accum = accum + jnp.mean(row_grad * row_grad, axis=-1)
     new_table = table - LEARN_RATE * row_grad / (jnp.sqrt(new_accum)[:, :, None] + EPSILON)
     return (dense_grad, new_table, new_accum)

time: 107 us -> 98.6 us (0.921)
  waiting for transfers between devices: 21.8 us -> 17.4 us
  starting transfers between devices: 27.8 us -> 24.7 us
    all_to_all x3 -> x2, waiting for transfers between devices: 19.1 us -> 14.8 us  [per_device(): lax.all_to_all(total.astype(jnp.bfloat16).reshape(outer * mp_count, len(c...]
    all_to_all x3 -> x2, starting transfers between devices: 11.7 us -> 8.55 us  [per_device(): lax.all_to_all(total.astype(jnp.bfloat16).reshape(outer * mp_count, len(c...]
  transfers between devices with their start and end apart: 8 -> 7, of which waited for: 5 -> 4; matrix products, arithmetic and copies ran while one was open for 31% -> 34% of each run, Pallas kernels for 15% -> 16%
where the time goes in v3:
time: 98.6 us; the launch traced here: 97.5 us
  starting transfers between devices  24.7 us (25%)
  local copies, waits for them, and re-layouts  20.2 us (20%)
  waiting for transfers between devices  17.4 us (18%)
  Pallas kernels  15.6 us (16%)
  matrix products  11.4 us (12%)
  other arithmetic  7.39 us (7%)
    pallas_call x4, Pallas kernels, sum_rows(): pl.pallas_call(sum_kernel, grid=(tables, blocks // step), in_specs=[pl.Bl...  15.6 us
    all_to_all x2, waiting for transfers between devices, per_device(): lax.all_to_all(total.astype(jnp.bfloat16).reshape(outer * mp_count, len(c...  14.8 us
    all_to_all x2, starting transfers between devices, per_device(): lax.all_to_all(total.astype(jnp.bfloat16).reshape(outer * mp_count, len(c...  8.55 us
    reshape x4, local copies, waits for them, and re-layouts, feature_grads(): symmetric = symmetric.reshape(batch_rows, len(wanted), feature_count)  7.93 us
    all_to_all x2, starting transfers between devices, per_device(): lax.all_to_all(send.reshape(mp_count, len(chunk), batch_rows, row_width),...  7.39 us
    unnamed x19, local copies, waits for them, and re-layouts  5.09 us
    dot_general x2, matrix products, feature_grads(): jnp.einsum('bh,zh->bz', top_cot, expanded, preferred_element_type=jnp.flo...  4.95 us
    dot_general x2, matrix products, feature_grads(): jnp.einsum('bij,bje->bie', symmetric, features, precision=lax.Precision.H...  4.58 us
  transfers between devices with their start and end apart: 7, of which 4 were waited for; matrix products, arithmetic and copies ran while one was open for 34% of the time, Pallas kernels for 16%

profile of v3, /device:TPU:0, one launch (start us, length us, event | category | flops | bytes accessed | tf_op | source)
XLA Modules:
  0.0 97.5 jit_solution(17735440361653758632)
XLA Ops:
  0.6 0.0 copy-start
  0.6 0.8 fusion.15
  1.5 0.6 copy.89
  2.1 4.3 %all-to-all-start = ((s32[4,7,256]{2,1,0:T(8,128)}), s32[4,7,256]{2,1,0:T(8,128)}, u32[]{:S(2)}, u32[]{:S(2)}) async-start(s32[4,7,256]{2,1,0:T(8,128)} %bitcast.49), calls=%async_computation | async-start | bytes 65536 | tf_op jit(solution)/shard_map/all_to_all | solution.py:87
  6.4 0.0 copy-done
  6.4 2.0 %fusion.5 = f32[256,351]{0,1:T(8,128)S(1)} fusion(bf16[256,1024]{1,0:T(8,128)(2,1)S(1)} %copy-done, bf16[351,351]{1,0:T(8,128)(2,1)} %constant.76.clone, bf16[479,1024]{1,0:T(8,128)(2,1)} %param.13), kind=kOutput, calls=%fused_computation.10 | convolution fusion | flops 436700160 | bytes 1874944 | tf_op jit(solution)/shard_map/bh,zh->bz/dot_general | solution.py:31
  8.5 2.5 %copy.66 = f32[256,13,27]{2,1,0:T(8,128)} copy(f32[256,13,27]{0,2,1:T(8,128)S(1)} %reshape.43) | data formatting | bytes 718848 | tf_op jit(solution)/shard_map/reshape | solution.py:32
  11.0 0.0 copy-start.7
  11.0 0.0 copy-start.1
  11.0 2.7 %copy.65 = bf16[256,26,128]{2,1,0:T(8,128)(2,1)S(1)} copy(bf16[256,26,128]{2,0,1:T(8,128)(2,1)} %param.10) | data formatting | bytes 3407872 | tf_op args[0]
  13.7 0.0 copy-done.7
  13.7 0.1 copy.64
  13.8 0.0 copy-done.1
  13.9 1.5 %fusion.2 = f32[256,13,128]{2,1,0:T(8,128)S(1)} fusion(f32[256,13,27]{2,1,0:T(8,128)S(1)} %copy-done.1, bf16[256,26,128]{2,1,0:T(8,128)(2,1)S(1)} %copy.65, bf16[256,1,128]{2,1,0:T(2,128)(2,1)S(1)} %copy.64), kind=kOutput, calls=%fused_computation.7 | convolution fusion | flops 72548352 | bytes 3832832 | tf_op jit(solution)/shard_map/bij,bje->bie/dot_general | solution.py:33
  15.4 0.0 copy-start.2
  15.4 1.3 %copy-done.2 = f32[256,13,128]{2,1,0:T(8,128)} copy-done((f32[256,13,128]{2,1,0:T(8,128)}, f32[256,13,128]{2,1,0:T(8,128)S(1)}, u32[]{:S(2)}) %copy-start.2) | copy-done | bytes 1703960
  16.7 0.1 fusion.7
  16.8 1.1 %copy.75 = bf16[12,256,128]{2,1,0:T(8,128)(2,1)} copy(bf16[12,256,128]{2,0,1:T(8,128)(2,1)S(1)} %fusion.7) | data formatting | bytes 1572864 | tf_op jit(solution)/shard_map/transpose | solution.py:113
  17.9 0.0 all-to-all-done
  17.9 3.9 %all-to-all-start.3 = ((bf16[4,3,256,128]{3,2,1,0:T(8,128)(2,1)}), bf16[4,3,256,128]{3,2,1,0:T(8,128)(2,1)S(1)}, u32[]{:S(2)}, u32[]{:S(2)}) async-start(bf16[4,3,256,128]{3,2,1,0:T(8,128)(2,1)} %bitcast.16), calls=%async_computation.3 | async-start | bytes 1572864 | tf_op jit(solution)/shard_map/all_to_all | solution.py:114
  21.8 2.9 %fusion.4 = f32[256,432]{0,1:T(8,128)} fusion(bf16[256,1024]{1,0:T(8,128)(2,1)S(1)} %copy-done, bf16[432,351]{1,0:T(8,128)(2,1)} %constant.75.clone, bf16[479,1024]{1,0:T(8,128)(2,1)} %param.13), kind=kOutput, calls=%fused_computation.9 | convolution fusion | flops 537477120 | bytes 2019328 | tf_op jit(solution)/shard_map/bh,zh->bz/dot_general | solution.py:31
  24.8 1.9 %reshape.45 = f32[256,16,27]{0,2,1:T(8,128)} reshape(f32[256,432]{0,1:T(8,128)} %fusion.4) | data formatting | bytes 884736 | tf_op jit(solution)/shard_map/reshape | solution.py:32
  26.6 3.5 %copy.70 = f32[256,16,27]{2,1,0:T(8,128)} copy(f32[256,16,27]{0,2,1:T(8,128)} %reshape.45) | data formatting | bytes 884736 | tf_op jit(solution)/shard_map/reshape | solution.py:32
  30.1 3.1 %fusion = bf16[16,256,128]{2,0,1:T(8,128)(2,1)S(1)} fusion(f32[256,16,27]{2,1,0:T(8,128)} %copy.70, bf16[256,26,128]{2,1,0:T(8,128)(2,1)S(1)} %copy.65, bf16[256,1,128]{2,1,0:T(2,128)(2,1)S(1)} %copy.64), kind=kOutput, calls=%fused_computation.5 | convolution fusion | flops 88997888 | bytes 3260416 | tf_op jit(solution)/shard_map/bij,bje->bie/dot_general | solution.py:33
  33.2 1.2 %copy.71 = bf16[16,256,128]{2,1,0:T(8,128)(2,1)} copy(bf16[16,256,128]{2,0,1:T(8,128)(2,1)S(1)} %fusion) | data formatting | bytes 2097152 | tf_op jit(solution)/shard_map/convert_element_type | solution.py:113
  34.5 0.0 all-to-all-done.3.rows_ref
  34.5 0.0 copy-start.4
  34.5 3.5 %all-to-all-start.1 = ((bf16[4,4,256,128]{3,2,1,0:T(8,128)(2,1)}), bf16[4,4,256,128]{3,2,1,0:T(8,128)(2,1)S(1)}, u32[]{:S(2)}, u32[]{:S(2)}) async-start(bf16[4,4,256,128]{3,2,1,0:T(8,128)(2,1)} %bitcast.9), calls=%async_computation.1 | async-start | bytes 2097152 | tf_op jit(solution)/shard_map/all_to_all | solution.py:114
  38.0 0.8 and_select_fusion
  38.8 0.6 copy.78.ids_ref
  39.5 0.0 copy-done.4
  39.5 3.5 %shard_map.124 = bf16[4,4,3,32,128]{4,3,2,1,0:T(8,128)(2,1)} custom-call(s32[4,3,1,256]{3,2,1,0:T(1,128)} %copy.78.ids_ref, bf16[4,3,256,128]{3,2,1,0:T(8,128)(2,1)} %copy-done.4), custom_call_target="tpu_custom_call" | custom-call | flops 402653184 | bytes 1572864 | tf_op jit(solution)/shard_map/pallas_call | solution.py:53
  43.0 2.2 %collective-permute-start.1 = (bf16[4,4,3,32,128]{4,3,2,1,0:T(8,128)(2,1)}, bf16[4,4,3,32,128]{4,3,2,1,0:T(8,128)(2,1)S(1)}, u32[]{:S(2)}, u32[]{:S(2)}) collective-permute-start(bf16[4,4,3,32,128]{4,3,2,1,0:T(8,128)(2,1)} %shard_map.124), channel_id=1, source_target_pairs={{0,4},{4,0},{8,12},{12,8},{16,20},{20,16},{24,28},{28,24},{1,5},{5... | collective-permute-start | bytes 1179656 | tf_op jit(solution)/shard_map/ppermute | solution.py:125
  45.2 0.8 and_select_fusion.1
  46.1 0.6 copy.76.ids_ref
  46.7 0.6 broadcast_in_dim.21.ids_ref
  47.3 3.6 %shard_map.123 = f32[4,4,3,32,128]{4,3,2,1,0:T(8,128)} custom-call(s32[4,3,1,256]{3,2,1,0:T(1,128)} %copy.76.ids_ref, bf16[4,3,256,128]{3,2,1,0:T(8,128)(2,1)} %copy-done.4), custom_call_target="tpu_custom_call" | custom-call | flops 402653184 | bytes 1572864 | tf_op jit(solution)/shard_map/pallas_call | solution.py:53
  51.0 0.0 copy-start.5
  51.0 1.5 %all-to-all-done.1.rows_ref = bf16[4,4,256,128]{3,2,1,0:T(8,128)(2,1)S(1)} async-done(((bf16[4,4,256,128]{3,2,1,0:T(8,128)(2,1)}), bf16[4,4,256,128]{3,2,1,0:T(8,128)(2,1)S(1)}, u32[]{:S(2)}, u32[]{:S(2)}) %all-to-all-start.1) | async-done | bytes 1048608 | tf_op jit(solution)/shard_map/all_to_all | solution.py:114
  52.4 1.0 copy-done.3
  53.4 4.2 %shard_map.122 = bf16[4,4,4,32,128]{4,3,2,1,0:T(8,128)(2,1)} custom-call(s32[4,4,1,256]{3,2,1,0:T(1,128)} %broadcast_in_dim.21.ids_ref, bf16[4,4,256,128]{3,2,1,0:T(8,128)(2,1)} %copy-done.3), custom_call_target="tpu_custom_call" | custom-call | flops 536870912 | bytes 2097152 | tf_op jit(solution)/shard_map/pallas_call | solution.py:53
  57.6 2.2 %collective-permute-start = (bf16[4,4,4,32,128]{4,3,2,1,0:T(8,128)(2,1)}, bf16[4,4,4,32,128]{4,3,2,1,0:T(8,128)(2,1)S(1)}, u32[]{:S(2)}, u32[]{:S(2)}) collective-permute-start(bf16[4,4,4,32,128]{4,3,2,1,0:T(8,128)(2,1)} %shard_map.122), channel_id=1, source_target_pairs={{0,4},{4,0},{8,12},{12,8},{16,20},{20,16},{24,28},{28,24},{1,5},{5... | collective-permute-start | bytes 1572872 | tf_op jit(solution)/shard_map/ppermute | solution.py:125
  59.8 0.0 collective-permute-done.1
  59.8 0.0 copy-done.5
  59.8 0.9 add_convert_fusion.1
  60.7 5.0 %all-to-all-start.4 = ((bf16[16,3,32,128]{3,2,1,0:T(8,128)(2,1)}), bf16[16,3,32,128]{3,2,1,0:T(8,128)(2,1)S(1)}, u32[]{:S(2)}, u32[]{:S(2)}) async-start(bf16[16,3,32,128]{3,2,1,0:T(8,128)(2,1)} %bitcast.18), calls=%async_computation.4 | async-start | bytes 786432 | tf_op jit(solution)/shard_map/all_to_all | solution.py:126
  65.6 0.6 copy.72.ids_ref
  66.3 4.2 %shard_map.121 = f32[4,4,4,32,128]{4,3,2,1,0:T(8,128)} custom-call(s32[4,4,1,256]{3,2,1,0:T(1,128)} %copy.72.ids_ref, bf16[4,4,256,128]{3,2,1,0:T(8,128)(2,1)} %copy-done.3), custom_call_target="tpu_custom_call" | custom-call | flops 536870912 | bytes 2097152 | tf_op jit(solution)/shard_map/pallas_call | solution.py:53
  70.5 1.1 %collective-permute-done = bf16[4,4,4,32,128]{4,3,2,1,0:T(8,128)(2,1)S(1)} collective-permute-done((bf16[4,4,4,32,128]{4,3,2,1,0:T(8,128)(2,1)}, bf16[4,4,4,32,128]{4,3,2,1,0:T(8,128)(2,1)S(1)}, u32[]{:S(2)}, u32[]{:S(2)}) %collective-permute-start) | collective-permute-done | bytes 524320 | tf_op jit(solution)/shard_map/ppermute | solution.py:125
  71.6 2.2 %add_convert_fusion = bf16[4,4,4,32,128]{4,3,2,1,0:T(8,128)(2,1)} fusion(f32[4,4,4,32,128]{4,3,2,1,0:T(8,128)} %shard_map.121, bf16[4,4,4,32,128]{4,3,2,1,0:T(8,128)(2,1)S(1)} %collective-permute-done), kind=kLoop, calls=%fused_computation.15 | loop fusion | flops 786432 | bytes 2097152 | tf_op jit(solution)/shard_map/convert_element_type | solution.py:127
  73.8 4.0 %all-to-all-done.4 = bf16[16,3,32,128]{3,2,1,0:T(8,128)(2,1)S(1)} async-done(((bf16[16,3,32,128]{3,2,1,0:T(8,128)(2,1)}), bf16[16,3,32,128]{3,2,1,0:T(8,128)(2,1)S(1)}, u32[]{:S(2)}, u32[]{:S(2)}) %all-to-all-start.4) | async-done | bytes 393248 | tf_op jit(solution)/shard_map/all_to_all | solution.py:126
  77.8 3.6 %all-to-all-start.2 = ((bf16[16,4,32,128]{3,2,1,0:T(8,128)(2,1)}), bf16[16,4,32,128]{3,2,1,0:T(8,128)(2,1)S(1)}, u32[]{:S(2)}, u32[]{:S(2)}) async-start(bf16[16,4,32,128]{3,2,1,0:T(8,128)(2,1)} %bitcast.10), calls=%async_computation.2 | async-start | bytes 1048576 | tf_op jit(solution)/shard_map/all_to_all | solution.py:126
  81.4 0.0 copy-start.8
  81.4 0.0 copy-start.6
  81.4 1.4 %slice.37 = f32[256,1,128]{2,1,0:T(1,128)S(1)} slice(f32[256,13,128]{2,1,0:T(8,128)} %copy-done.2), slice={[0:256], [12:13], [0:128]} | slice | bytes 262144 | tf_op jit(solution)/shard_map/slice | solution.py:111
  82.8 1.9 %fusion.6 = bf16[256,128]{1,0:T(8,128)(2,1)} fusion(f32[256,128]{1,0:T(8,128)S(1)} %bitcast.58, bf16[256,1024]{1,0:T(8,128)(2,1)S(1)} %copy-done, bf16[479,1024]{1,0:T(8,128)(2,1)} %param.13), kind=kOutput, calls=%fused_computation.12 | convolution fusion | flops 67174400 | bytes 983040 | tf_op jit(solution)/shard_map/bh,zh->bz/dot_general | solution.py:108
  84.7 0.1 convert_reduce_fusion.1
  84.8 10.9 %all-to-all-done.2 = bf16[16,4,32,128]{3,2,1,0:T(8,128)(2,1)S(1)} async-done(((bf16[16,4,32,128]{3,2,1,0:T(8,128)(2,1)}), bf16[16,4,32,128]{3,2,1,0:T(8,128)(2,1)S(1)}, u32[]{:S(2)}, u32[]{:S(2)}) %all-to-all-start.2) | async-done | bytes 524320 | tf_op jit(solution)/shard_map/all_to_all | solution.py:126
  95.6 0.1 convert_reduce_fusion
  95.7 0.2 multiply_reduce_fusion
  95.9 0.0 copy-done.8
  95.9 0.6 sqrt_add_fusion
  96.5 0.0 copy-done.6
  96.5 0.9 divide_subtract_fusion
  (10 shorter events, 0.1 us)
Async XLA Ops:
  0.6 5.8 %copy-start = (bf16[256,1024]{1,0:T(8,128)(2,1)S(1)}, bf16[256,1024]{1,0:T(8,128)(2,1)}, u32[]{:S(2)}) copy-start(bf16[256,1024]{1,0:T(8,128)(2,1)} %param.12) | copy-start | bytes 1572868
  2.1 15.8 %all-to-all-start = ((s32[4,7,256]{2,1,0:T(8,128)}), s32[4,7,256]{2,1,0:T(8,128)}, u32[]{:S(2)}, u32[]{:S(2)}) async-start(s32[4,7,256]{2,1,0:T(8,128)} %bitcast.49), calls=%async_computation | async-start | bytes 65536 | tf_op jit(solution)/shard_map/all_to_all | solution.py:87
  11.0 2.8 %copy-start.7 = (bf16[256,128]{1,0:T(8,128)(2,1)S(1)}, bf16[256,128]{1,0:T(8,128)(2,1)}, u32[]{:S(2)}) copy-start(bf16[256,128]{1,0:T(8,128)(2,1)} %param.11) | copy-start | bytes 196612
  11.0 2.9 %copy-start.1 = (f32[256,13,27]{2,1,0:T(8,128)S(1)}, f32[256,13,27]{2,1,0:T(8,128)}, u32[]{:S(2)}) copy-start(f32[256,13,27]{2,1,0:T(8,128)} %copy.66) | copy-start | bytes 1078276
  15.4 1.3 %copy-start.2 = (f32[256,13,128]{2,1,0:T(8,128)}, f32[256,13,128]{2,1,0:T(8,128)S(1)}, u32[]{:S(2)}) copy-start(f32[256,13,128]{2,1,0:T(8,128)S(1)} %fusion.2) | copy-start | bytes 5111812
  17.9 16.5 %all-to-all-start.3 = ((bf16[4,3,256,128]{3,2,1,0:T(8,128)(2,1)}), bf16[4,3,256,128]{3,2,1,0:T(8,128)(2,1)S(1)}, u32[]{:S(2)}, u32[]{:S(2)}) async-start(bf16[4,3,256,128]{3,2,1,0:T(8,128)(2,1)} %bitcast.16), calls=%async_computation.3 | async-start | bytes 1572864 | tf_op jit(solution)/shard_map/all_to_all | solution.py:114
  34.5 5.0 %copy-start.4 = (bf16[4,3,256,128]{3,2,1,0:T(8,128)(2,1)}, bf16[4,3,256,128]{3,2,1,0:T(8,128)(2,1)S(1)}, u32[]{:S(2)}) copy-start(bf16[4,3,256,128]{3,2,1,0:T(8,128)(2,1)S(1)} %all-to-all-done.3.rows_ref) | copy-start | bytes 2359300
  34.5 17.9 %all-to-all-start.1 = ((bf16[4,4,256,128]{3,2,1,0:T(8,128)(2,1)}), bf16[4,4,256,128]{3,2,1,0:T(8,128)(2,1)S(1)}, u32[]{:S(2)}, u32[]{:S(2)}) async-start(bf16[4,4,256,128]{3,2,1,0:T(8,128)(2,1)} %bitcast.9), calls=%async_computation.1 | async-start | bytes 2097152 | tf_op jit(solution)/shard_map/all_to_all | solution.py:114
  43.0 16.8 %collective-permute-start.1 = (bf16[4,4,3,32,128]{4,3,2,1,0:T(8,128)(2,1)}, bf16[4,4,3,32,128]{4,3,2,1,0:T(8,128)(2,1)S(1)}, u32[]{:S(2)}, u32[]{:S(2)}) collective-permute-start(bf16[4,4,3,32,128]{4,3,2,1,0:T(8,128)(2,1)} %shard_map.124), channel_id=1, source_target_pairs={{0,4},{4,0},{8,12},{12,8},{16,20},{20,16},{24,28},{28,24},{1,5},{5... | collective-permute-start | bytes 1179656 | tf_op jit(solution)/shard_map/ppermute | solution.py:125
  51.0 8.8 %copy-start.5 = (f32[4,4,3,32,128]{4,3,2,1,0:T(8,128)S(1)}, f32[4,4,3,32,128]{4,3,2,1,0:T(8,128)}, u32[]{:S(2)}) copy-start(f32[4,4,3,32,128]{4,3,2,1,0:T(8,128)} %shard_map.123) | copy-start | bytes 2359300
  52.4 1.0 copy-start.3
  57.6 14.1 %collective-permute-start = (bf16[4,4,4,32,128]{4,3,2,1,0:T(8,128)(2,1)}, bf16[4,4,4,32,128]{4,3,2,1,0:T(8,128)(2,1)S(1)}, u32[]{:S(2)}, u32[]{:S(2)}) collective-permute-start(bf16[4,4,4,32,128]{4,3,2,1,0:T(8,128)(2,1)} %shard_map.122), channel_id=1, source_target_pairs={{0,4},{4,0},{8,12},{12,8},{16,20},{20,16},{24,28},{28,24},{1,5},{5... | collective-permute-start | bytes 1572872 | tf_op jit(solution)/shard_map/ppermute | solution.py:125
  60.7 17.1 %all-to-all-start.4 = ((bf16[16,3,32,128]{3,2,1,0:T(8,128)(2,1)}), bf16[16,3,32,128]{3,2,1,0:T(8,128)(2,1)S(1)}, u32[]{:S(2)}, u32[]{:S(2)}) async-start(bf16[16,3,32,128]{3,2,1,0:T(8,128)(2,1)} %bitcast.18), calls=%async_computation.4 | async-start | bytes 786432 | tf_op jit(solution)/shard_map/all_to_all | solution.py:126
  77.8 17.8 %all-to-all-start.2 = ((bf16[16,4,32,128]{3,2,1,0:T(8,128)(2,1)}), bf16[16,4,32,128]{3,2,1,0:T(8,128)(2,1)S(1)}, u32[]{:S(2)}, u32[]{:S(2)}) async-start(bf16[16,4,32,128]{3,2,1,0:T(8,128)(2,1)} %bitcast.10), calls=%async_computation.2 | async-start | bytes 1048576 | tf_op jit(solution)/shard_map/all_to_all | solution.py:126
  81.4 14.5 %copy-start.8 = (f32[26,32]{1,0:T(8,128)S(1)}, f32[26,32]{1,0:T(8,128)}, u32[]{:S(2)}) copy-start(f32[26,32]{1,0:T(8,128)} %param.17) | copy-start | bytes 9988
  81.4 15.1 %copy-start.6 = (f32[26,32,128]{2,1,0:T(8,128)S(1)}, f32[26,32,128]{2,1,0:T(8,128)}, u32[]{:S(2)}) copy-start(f32[26,32,128]{2,1,0:T(8,128)} %param.16) | copy-start | bytes 1277956
